TPU v7x, 32 devices: a 4x2x2 block of a 4x4x8 slice. The times are simulated.
32 devices in a mesh: dp: 4 (over y, z), tp: 8 (over x, core).
Axes of the slice: x: 4, y: 2, z: 2, core: 2. Of those that a mesh axis runs over, the one named last changes fastest.
The devices are a block of a 4x4x8 slice.
Arguments:
- x: bfloat16 [32, 576, 1024], P('dp', 'tp'), parts along dimension 0
- d_out: bfloat16 [32, 576, 1024], P('dp', 'tp'), parts along dimension 0
- ln1_gain: float32 [1024], replicated
- ln1_bias: float32 [1024], replicated
- w_q: bfloat16 [1024, 16, 64], P(None, 'tp')
- b_q: bfloat16 [16, 64], P('tp')
- w_k: bfloat16 [1024, 16, 64], P(None, 'tp')
- w_v: bfloat16 [1024, 16, 64], P(None, 'tp')
- b_v: bfloat16 [16, 64], P('tp')
- w_o: bfloat16 [16, 64, 1024], P('tp')
- b_o: bfloat16 [1024], replicated
- ln2_gain: float32 [1024], replicated
- ln2_bias: float32 [1024], replicated
- w_1: bfloat16 [1024, 4096], P(None, 'tp')
- b_1: bfloat16 [4096], P('tp')
- w_2: bfloat16 [4096, 1024], P('tp')
- b_2: bfloat16 [1024], replicated
Outputs:
- output 1: bfloat16 [32, 576, 1024], P('dp', 'tp'), parts along dimension 0
- output 2: bfloat16 [32, 576, 1024], P('dp', 'tp'), parts along dimension 0
- output 3: float32 [4096], P('dp'), parts along dimension 0
- output 4: float32 [4096], P('dp'), parts along dimension 0
- output 5: bfloat16 [4096, 16, 64], P('dp', 'tp'), parts along dimension 0
- output 6: bfloat16 [64, 64], P(('dp', 'tp')), parts along dimension 0
- output 7: bfloat16 [4096, 16, 64], P('dp', 'tp'), parts along dimension 0
- output 8: bfloat16 [4096, 16, 64], P('dp', 'tp'), parts along dimension 0
- output 9: bfloat16 [64, 64], P(('dp', 'tp')), parts along dimension 0
- output 10: bfloat16 [64, 64, 1024], P(('dp', 'tp')), parts along dimension 0
- output 11: bfloat16 [4096], P('dp'), parts along dimension 0
- output 12: float32 [4096], P('dp'), parts along dimension 0
- output 13: float32 [4096], P('dp'), parts along dimension 0
- output 14: bfloat16 [4096, 4096], P('dp', 'tp'), parts along dimension 0
- output 15: bfloat16 [16384], P(('dp', 'tp')), parts along dimension 0
- output 16: bfloat16 [16384, 1024], P(('dp', 'tp')), parts along dimension 0
- output 17: bfloat16 [4096], P('dp'), parts along dimension 0
There are 4 independent parts. A program takes and returns all parts, laid end to end along the dimension named above; an argument that names none is the same for every part.
All inputs are finite; a program needn't handle non-finite values.
Results may differ from a plain program's by a relative error of at most 0.0187366.
Values are sent between devices in bfloat16 or wider.
A program may use at most 768 MiB of HBM per device.

v0:
```python
import math
import jax
import jax.numpy as jnp
from jax import lax
from jax.sharding import PartitionSpec as P

LN_EPS = 1e-6


def layer_norm(rows, ln_gain, ln_bias):
    row_mean = jnp.mean(rows, axis=-1, keepdims=True)
    centered = rows - row_mean
    variance = jnp.mean(centered * centered, axis=-1, keepdims=True)
    return centered * lax.rsqrt(variance + LN_EPS) * ln_gain + ln_bias


def gelu_tanh(pre_act):
    return jax.nn.gelu(pre_act, approximate=True)


def attention_core(queries, keys, values):
    att_scale = 1.0 / math.sqrt(queries.shape[-1])
    scores = jnp.einsum('bqhd,bkhd->bhqk', queries, keys, preferred_element_type=jnp.float32) * att_scale
    probs = jax.nn.softmax(scores, axis=-1).astype(jnp.bfloat16)
    mixed = jnp.einsum('bhqk,bkhd->bqhd', probs, values, preferred_element_type=jnp.float32)
    return mixed.astype(jnp.bfloat16)


def token_sum(grad_rows):
    return jnp.sum(grad_rows, axis=(0, 1), dtype=jnp.float32)


def solution(mesh):
    act_spec = P('dp', 'tp', None)
    replicated = P()
    head_w = P(None, 'tp', None)
    head_b = P('tp', None)
    grad_head_w = P('dp', 'tp', None)
    grad_head_b = P(('dp', 'tp'), None)
    grad_vec = P('dp')
    in_specs = (act_spec, act_spec, replicated, replicated, head_w, head_b, head_w, head_w, head_b,
                P('tp', None, None), replicated, replicated, replicated, P(None, 'tp'), P('tp'), P('tp', None), replicated)
    out_specs = (act_spec, act_spec, grad_vec, grad_vec, grad_head_w, grad_head_b, grad_head_w, grad_head_w, grad_head_b,
                 P(('dp', 'tp'), None, None), grad_vec, grad_vec, grad_vec, P('dp', 'tp'), P(('dp', 'tp')),
                 P(('dp', 'tp'), None), grad_vec)

    def gather_tokens(local_rows):
        return lax.all_gather(local_rows, 'tp', axis=1, tiled=True)

    def scatter_sum(part_sum):
        return lax.psum_scatter(part_sum, 'tp', scatter_dimension=1, tiled=True)

    def layer_step(x, d_out, ln1_gain, ln1_bias, w_q, b_q, w_k, w_v, b_v, w_o, b_o, ln2_gain, ln2_bias, w_1, b_1, w_2, b_2):
        x_f32 = x.astype(jnp.float32)
        h_one_f, ln1_pull = jax.vjp(layer_norm, x_f32, ln1_gain, ln1_bias)
        h_one = gather_tokens(h_one_f.astype(jnp.bfloat16))
        queries = (jnp.einsum('bnw,whd->bnhd', h_one, w_q, preferred_element_type=jnp.float32) + b_q).astype(jnp.bfloat16)
        keys = jnp.einsum('bnw,whd->bnhd', h_one, w_k, preferred_element_type=jnp.float32).astype(jnp.bfloat16)
        values = (jnp.einsum('bnw,whd->bnhd', h_one, w_v, preferred_element_type=jnp.float32) + b_v).astype(jnp.bfloat16)
        mixed, attn_pull = jax.vjp(attention_core, queries, keys, values)
        attn_out = scatter_sum(jnp.einsum('bnhd,hdw->bnw', mixed, w_o, preferred_element_type=jnp.float32))
        x_mid = (x_f32 + attn_out + b_o).astype(jnp.bfloat16)
        mid_f32 = x_mid.astype(jnp.float32)
        h_two_f, ln2_pull = jax.vjp(layer_norm, mid_f32, ln2_gain, ln2_bias)
        h_two = gather_tokens(h_two_f.astype(jnp.bfloat16))
        pre_act = (jnp.einsum('bnw,wf->bnf', h_two, w_1, preferred_element_type=jnp.float32) + b_1).astype(jnp.bfloat16)
        hidden_f, gelu_pull = jax.vjp(gelu_tanh, pre_act.astype(jnp.float32))
        hidden = hidden_f.astype(jnp.bfloat16)
        mlp_out = scatter_sum(jnp.einsum('bnf,fw->bnw', hidden, w_2, preferred_element_type=jnp.float32))
        y_out = (mid_f32 + mlp_out + b_2).astype(jnp.bfloat16)

        d_out_all = gather_tokens(d_out)
        d_hidden = jnp.einsum('bnw,fw->bnf', d_out_all, w_2, preferred_element_type=jnp.float32).astype(jnp.bfloat16)
        grad_w_2 = jnp.einsum('bnf,bnw->fw', hidden, d_out_all, preferred_element_type=jnp.float32).astype(jnp.bfloat16)
        (d_pre_f,) = gelu_pull(d_hidden.astype(jnp.float32))
        d_pre = d_pre_f.astype(jnp.bfloat16)
        grad_b_1 = token_sum(d_pre).astype(jnp.bfloat16)
        grad_w_1 = jnp.einsum('bnw,bnf->wf', h_two, d_pre, preferred_element_type=jnp.float32).astype(jnp.bfloat16)
        d_h_two = scatter_sum(jnp.einsum('bnf,wf->bnw', d_pre, w_1, preferred_element_type=jnp.float32)).astype(jnp.bfloat16)
        d_mid_ln, g_ln2_gain, g_ln2_bias = ln2_pull(d_h_two.astype(jnp.float32))
        d_mid = (d_out.astype(jnp.float32) + d_mid_ln).astype(jnp.bfloat16)
        d_mid_all = gather_tokens(d_mid)
        d_mixed = jnp.einsum('bnw,hdw->bnhd', d_mid_all, w_o, preferred_element_type=jnp.float32).astype(jnp.bfloat16)
        grad_w_o = jnp.einsum('bnhd,bnw->hdw', mixed, d_mid_all, preferred_element_type=jnp.float32).astype(jnp.bfloat16)
        d_query, d_key, d_value = attn_pull(d_mixed)
        grad_b_q = token_sum(d_query).astype(jnp.bfloat16)
        grad_b_v = token_sum(d_value).astype(jnp.bfloat16)
        grad_w_q = jnp.einsum('bnw,bnhd->whd', h_one, d_query, preferred_element_type=jnp.float32).astype(jnp.bfloat16)
        grad_w_k = jnp.einsum('bnw,bnhd->whd', h_one, d_key, preferred_element_type=jnp.float32).astype(jnp.bfloat16)
        grad_w_v = jnp.einsum('bnw,bnhd->whd', h_one, d_value, preferred_element_type=jnp.float32).astype(jnp.bfloat16)
        d_h_one_part = (jnp.einsum('bnhd,whd->bnw', d_query, w_q, preferred_element_type=jnp.float32)
                        + jnp.einsum('bnhd,whd->bnw', d_key, w_k, preferred_element_type=jnp.float32)
                        + jnp.einsum('bnhd,whd->bnw', d_value, w_v, preferred_element_type=jnp.float32))
        d_h_one = scatter_sum(d_h_one_part).astype(jnp.bfloat16)
        d_in_ln, g_ln1_gain, g_ln1_bias = ln1_pull(d_h_one.astype(jnp.float32))
        grad_x = (d_mid.astype(jnp.float32) + d_in_ln).astype(jnp.bfloat16)
        vec_sums = lax.psum(jnp.stack([g_ln1_gain, g_ln1_bias, token_sum(d_mid), g_ln2_gain, g_ln2_bias, token_sum(d_out)]), 'tp')
        return (y_out, grad_x, vec_sums[0], vec_sums[1], grad_w_q, grad_b_q, grad_w_k, grad_w_v, grad_b_v, grad_w_o,
                vec_sums[2].astype(jnp.bfloat16), vec_sums[3], vec_sums[4], grad_w_1, grad_b_1, grad_w_2,
                vec_sums[5].astype(jnp.bfloat16))

    return jax.shard_map(layer_step, mesh=mesh, in_specs=in_specs, out_specs=out_specs, check_vma=False)
```

profile of v0, /device:TPU:81, one launch (start us, length us, event | category | flops | bytes accessed | tf_op | source)
XLA Modules:
  0.0 851.1 jit_solution(5794951864295552025)
XLA Ops:
  7.3 1.7 convert_reduce_fusion.3
  9.0 1.8 fusion.57
  12.0 1.5 fusion.54
  13.7 55.4 %all-gather.5.cloned.1.call-done = bf16[8,576,1024]{2,1,0:T(8,128)(2,1)} async-done(((bf16[8,72,1024]{2,1,0:T(8,128)(2,1)}), bf16[8,576,1024]{2,1,0:T(8,128)(2,1)}) %all-gather.5.cloned.1.call-update) | async-done | bytes 9437200 | tf_op jit(solution)/shard_map/all_gather | solution.py:48
  69.2 8.2 fusion.71
  77.3 4.3 add_convert_fusion.1
  81.6 13.5 %fusion.136 = (f32[8,2,576]{2,1,0:T(2,128)S(1)}, f32[8,2,576,576]{2,3,1,0:T(8,128)}) fusion(bf16[8,576,2,64]{1,3,2,0:T(8,128)(2,1)} %add_convert_fusion.1, bf16[8,576,2,64]{1,3,2,0:T(8,128)(2,1)} %fusion.71), kind=kOutput, calls=%fused_computation.154 | convolution fusion | flops 695403072 | bytes 23629824 | tf_op jit(solution)/shard_map/jvp()/sub | solution.py:24
  95.1 9.1 %divide_convert_fusion = bf16[8,2,576,576]{2,3,1,0:T(8,128)(2,1)S(1)} fusion(f32[8,2,576,576]{2,3,1,0:T(8,128)} %get-tuple-element.40, f32[8,2,576]{2,1,0:T(2,128)S(1)} %get-tuple-element.39), kind=kLoop, calls=%fused_computation.8 | loop fusion | flops 10616832 | bytes 31887360 | tf_op jit(solution)/shard_map/jvp()/convert_element_type | solution.py:24
  104.3 11.2 %add_convert_fusion.2 = bf16[8,576,2,64]{1,3,2,0:T(8,128)(2,1)S(1)} fusion(bf16[8,576,1024]{2,1,0:T(8,128)(2,1)} %all-gather.5.cloned.1.call-done, f32[2,64]{1,0:T(2,128)S(1)} %convert_element_type.161, bf16[1024,2,64]{0,2,1:T(8,128)(2,1)S(1)} %copy-done.20), kind=kOutput, calls=%fused_computation.83 | convolution fusion | flops 1209139200 | bytes 10879488 | tf_op jit(solution)/shard_map/bnw,whd->bnhd/dot_general | solution.py:59
  115.5 2.2 fusion.79
  117.7 1.0 copy-done.5
  118.8 7.8 convolution_bitcast_fusion
  127.3 97.5 %reduce-scatter.5.cloned.1.call-done = f32[8,72,1024]{2,1,0:T(8,128)} async-done(((f32[8,576,1024]{2,1,0:T(8,128)}), f32[8,72,1024]{2,1,0:T(8,128)}) %reduce-scatter.5.cloned.1.call-update) | async-done | bytes 2359312 | tf_op jit(solution)/shard_map/reduce_scatter | solution.py:51
  224.8 2.1 convert_reduce_fusion.2
  227.5 1.5 fusion.52
  229.8 50.8 %all-gather.7.cloned.1.call-done = bf16[8,576,1024]{2,1,0:T(8,128)(2,1)} async-done(((bf16[8,72,1024]{2,1,0:T(8,128)(2,1)}), bf16[8,576,1024]{2,1,0:T(8,128)(2,1)}) %all-gather.7.cloned.1.call-update) | async-done | bytes 9437200 | tf_op jit(solution)/shard_map/all_gather | solution.py:48
  280.6 10.5 %add_convert_fusion = bf16[8,576,512]{2,1,0:T(8,128)(2,1)} fusion(f32[512]{0:T(512)S(1)} %convert_element_type.173, bf16[8,576,1024]{2,1,0:T(8,128)(2,1)} %all-gather.7.cloned.1.call-done, bf16[1024,512]{1,0:T(8,128)(2,1)S(1)} %copy-done.41), kind=kOutput, calls=%fused_computation.49 | convolution fusion | flops 4836556800 | bytes 15206400 | tf_op jit(solution)/shard_map/bnw,wf->bnf/dot_general | solution.py:66
  291.1 42.1 %all-gather.9.cloned.1.call-done = bf16[8,576,1024]{2,1,0:T(8,128)(2,1)} async-done(((bf16[8,72,1024]{2,1,0:T(8,128)(2,1)}), bf16[8,576,1024]{2,1,0:T(8,128)(2,1)}) %all-gather.9.cloned.1.call-update) | async-done | bytes 9437200 | tf_op jit(solution)/shard_map/all_gather | solution.py:48
  333.2 15.2 %fusion.139 = (bf16[512]{0:T(512)(128)(2,1)}, bf16[8,576,512]{2,1,0:T(8,128)(2,1)S(1)}) fusion(bf16[8,576,512]{2,1,0:T(8,128)(2,1)} %add_convert_fusion, bf16[8,576,1024]{2,1,0:T(8,128)(2,1)} %all-gather.9.cloned.1.call-done, bf16[512,1024]{1,0:T(8,128)(2,1)S(1)} %copy-done), kind=kOutput, calls=%fused_computation.157 | convolution fusion | flops 4888460800 | bytes 19923968 | tf_op jit(solution)/shard_map/bnw,fw->bnf/dot_general | solution.py:73
  348.4 2.2 copy-done.44
  350.6 9.5 %fusion.113 = f32[8,576,1024]{2,1,0:T(8,128)} fusion(bf16[8,576,512]{2,1,0:T(8,128)(2,1)S(1)} %get-tuple-element.48, bf16[1024,512]{1,0:T(8,128)(2,1)S(1)} %copy-done.41), kind=kOutput, calls=%fused_computation.126 | convolution fusion | flops 4831838208 | bytes 24641536 | tf_op jit(solution)/shard_map/bnf,wf->bnw/dot_general | solution.py:79
  360.2 13.7 %fusion.111 = f32[8,576,1024]{2,1,0:T(8,128)} fusion(bf16[512,1024]{1,0:T(8,128)(2,1)S(1)} %copy-done, bf16[8,576,512]{2,1,0:T(8,128)(2,1)} %add_convert_fusion), kind=kOutput, calls=%fused_computation.124 | convolution fusion | flops 4855431168 | bytes 24641536 | tf_op jit(solution)/shard_map/bnf,fw->bnw/dot_general | solution.py:69
  374.6 83.7 %reduce-scatter.9.cloned.1.call-done = f32[8,72,1024]{2,1,0:T(8,128)} async-done(((f32[8,576,1024]{2,1,0:T(8,128)}), f32[8,72,1024]{2,1,0:T(8,128)}) %reduce-scatter.9.cloned.1.call-update) | async-done | bytes 2359312 | tf_op jit(solution)/shard_map/reduce_scatter | solution.py:51
  458.3 2.9 convert_reduce_fusion.1
  461.2 1.9 fusion.65
  463.1 95.7 %reduce-scatter.7.cloned.1.call-done = f32[8,72,1024]{2,1,0:T(8,128)} async-done(((f32[8,576,1024]{2,1,0:T(8,128)}), f32[8,72,1024]{2,1,0:T(8,128)}) %reduce-scatter.7.cloned.1.call-update) | async-done | bytes 2359312 | tf_op jit(solution)/shard_map/reduce_scatter | solution.py:51
  558.8 4.5 convert_reduce_fusion.4
  563.5 51.4 %all-gather.11.cloned.1.call-done = bf16[8,576,1024]{2,1,0:T(8,128)(2,1)} async-done(((bf16[8,72,1024]{2,1,0:T(8,128)(2,1)}), bf16[8,576,1024]{2,1,0:T(8,128)(2,1)}) %all-gather.11.cloned.1.call-update) | async-done | bytes 9437200 | tf_op jit(solution)/shard_map/all_gather | solution.py:48
  614.9 7.0 fusion.83
  621.9 1.0 copy-done.10
  622.9 8.5 fusion.138
  631.4 15.5 %fusion.5 = (f32[8,2,576]{2,1,0:T(2,128)S(1)}, bf16[8,2,576,576]{2,3,1,0:T(8,128)(2,1)}) fusion(f32[8,2,576,576]{2,3,1,0:T(8,128)} %get-tuple-element.40, f32[8,2,576]{2,1,0:T(2,128)S(1)} %multiply_divide_fusion, bf16[8,2,64,576]{3,2,1,0:T(8,128)(2,1)} %copy-done.10, bf16[8,576,2,64]{1,3,2,0:T(8,128)(2,1)} %copy-done.9), kind=kOutput, calls=%fused_computation.7 | convolution fusion | flops 706010112 | bytes 34283520 | tf_op jit(solution)/shard_map/transpose(jvp(bhqk,bkhd->bqhd))/dot_general | solution.py:25
  646.9 15.0 %fusion.82 = bf16[8,576,2,64]{1,3,2,0:T(8,128)(2,1)} fusion(bf16[8,576,2,64]{1,3,2,0:T(8,128)(2,1)} %add_convert_fusion.1, f32[8,2,576,576]{2,3,1,0:T(8,128)} %get-tuple-element.40, bf16[8,2,576,576]{2,3,1,0:T(8,128)(2,1)} %get-tuple-element.42, f32[8,2,576]{2,1,0:T(2,128)S(1)} %neg.13, f32[8,2,576]{2,1,0:T(2,128)S(1)} %get-tuple-element.39), kind=kOutput, calls=%fused_computation.113 | convolution fusion | flops 706609152 | bytes 34283520 | tf_op jit(solution)/shard_map/transpose(jvp(bqhd,bkhd->bhqk))/dot_general | solution.py:23
  661.9 15.6 %fusion.137 = (bf16[2,64]{1,0:T(2,128)(2,1)}, bf16[8,576,2,64]{1,3,2,0:T(8,128)(2,1)}) fusion(bf16[8,576,2,64]{1,3,2,0:T(8,128)(2,1)} %fusion.71, f32[8,2,576,576]{2,3,1,0:T(8,128)} %get-tuple-element.40, bf16[8,2,576,576]{2,3,1,0:T(8,128)(2,1)} %get-tuple-element.42, f32[8,2,576]{2,1,0:T(2,128)S(1)} %neg.13, f32[8,2,576]{2,1,0:T(2,128)S(1)} %get-tuple-element.39), kind=kOutput, calls=%fused_computation.155 | convolution fusion | flops 707198848 | bytes 34283776 | tf_op jit(solution)/shard_map/transpose(jvp(bqhd,bkhd->bhqk))/dot_general | solution.py:23
  677.5 9.4 %fusion.118 = f32[8,576,1024,1]{2,1,3,0:T(8,128)} fusion(bf16[8,576,2,64]{1,3,2,0:T(8,128)(2,1)} %fusion.82, bf16[1024,2,64]{0,2,1:T(8,128)(2,1)S(1)} %copy-done.17), kind=kOutput, calls=%fused_computation.131 | convolution fusion | flops 1207959552 | bytes 20316160 | tf_op jit(solution)/shard_map/bnhd,whd->bnw/dot_general | solution.py:92
  686.9 7.9 fusion.121
  694.8 20.2 %bitcast_add_fusion = f32[8,576,1024]{2,1,0:T(8,128)} fusion(f32[8,576,1024,1]{2,1,3,0:T(8,128)} %fusion.118, f32[8,576,1024,1]{2,1,3,0:T(8,128)} %fusion.121, bf16[8,576,2,64]{1,3,2,0:T(8,128)(2,1)S(1)} %get-tuple-element.46, bf16[1024,2,64]{0,2,1:T(8,128)(2,1)S(1)} %copy-done.21), kind=kOutput, calls=%fused_computation.12 | convolution fusion | flops 1217396736 | bytes 58064896 | tf_op jit(solution)/shard_map/bnhd,whd->bnw/dot_general | solution.py:93
  715.1 10.1 %bitcast_convert_fusion.1 = bf16[1024,512]{1,0:T(8,128)(2,1)} fusion(bf16[8,576,1024]{2,1,0:T(8,128)(2,1)} %all-gather.7.cloned.1.call-done, bf16[8,576,512]{2,1,0:T(8,128)(2,1)} %copy-done.44), kind=kOutput, calls=%fused_computation.101 | convolution fusion | flops 4832362496 | bytes 15204352 | tf_op jit(solution)/shard_map/bnw,bnf->wf/dot_general | solution.py:78
  725.3 11.1 %bitcast_convert_fusion = bf16[512,1024]{1,0:T(8,128)(2,1)} fusion(bf16[8,576,1024]{2,1,0:T(8,128)(2,1)} %all-gather.9.cloned.1.call-done, bf16[8,576,512]{2,1,0:T(8,128)(2,1)} %add_convert_fusion), kind=kOutput, calls=%fused_computation.100 | convolution fusion | flops 4855955456 | bytes 15204352 | tf_op jit(solution)/shard_map/bnf,bnw->fw/dot_general | solution.py:74
  736.4 2.1 fusion.98
  738.6 2.2 fusion.101
  740.8 2.2 fusion.107
  743.0 2.2 fusion.104
  745.2 68.0 %reduce-scatter.11.cloned.1.call-done = f32[8,72,1024]{2,1,0:T(8,128)} async-done(((f32[8,576,1024]{2,1,0:T(8,128)}), f32[8,72,1024]{2,1,0:T(8,128)}) %reduce-scatter.11.cloned.1.call-update) | async-done | bytes 2359312 | tf_op jit(solution)/shard_map/reduce_scatter | solution.py:51
  813.2 2.3 convert_reduce_fusion
  816.6 1.5 fusion.66
  818.1 21.3 %psum.7 = f32[6,1024]{1,0:T(8,128)S(1)} all-reduce(f32[6,1024]{1,0:T(8,128)S(1)} %stack.27), channel_id=1, replica_groups=mesh['dp'=4,'tp'=8] {'tp'}, use_global_device_ids=true, to_apply=%region_21.0 | all-reduce | flops 6144 | bytes 49152 | tf_op jit(solution)/shard_map/psum | solution.py:97
  840.1 3.3 fusion.56
  (137 shorter events, 6.7 us)
Async XLA Ops:
  7.2 326.0 %copy-start = (bf16[512,1024]{1,0:T(8,128)(2,1)S(1)}, bf16[512,1024]{1,0:T(8,128)(2,1)}, u32[]{:S(2)}) copy-start(bf16[512,1024]{1,0:T(8,128)(2,1)} %param.32) | copy-start | bytes 3145732
  7.2 4.8 copy-start.3
  7.2 4.8 copy-start.25
  7.2 4.8 copy-start.35
  7.3 61.9 %all-gather.5.cloned.1.call-start = ((), (), s32[]{:S(2)}) async-start(), calls=%async_computation.4 | async-start | bytes 10616832 | tf_op jit(solution)/shard_map/all_gather | solution.py:48
  9.0 2.4 copy-start.22
  9.0 4.7 copy-start.42
  9.0 4.7 copy-start.43
  9.0 60.2 %copy-start.16 = (bf16[1024,2,64]{0,2,1:T(8,128)(2,1)S(1)}, bf16[1024,2,64]{0,2,1:T(8,128)(2,1)}, u32[]{:S(2)}) copy-start(bf16[1024,2,64]{0,2,1:T(8,128)(2,1)} %param.23) | copy-start | bytes 786436
  13.6 211.2 %reduce-scatter.5.cloned.1.call-start = ((), (), s32[]{:S(2)}) async-start(), calls=%async_computation.5 | async-start | bytes 21233664 | tf_op jit(solution)/shard_map/reduce_scatter | solution.py:51
  13.7 63.6 %copy-start.18 = (bf16[1024,2,64]{0,2,1:T(8,128)(2,1)S(1)}, bf16[1024,2,64]{0,2,1:T(8,128)(2,1)}, u32[]{:S(2)}) copy-start(bf16[1024,2,64]{0,2,1:T(8,128)(2,1)} %param.21) | copy-start | bytes 786436
  69.2 8.2 copy-start.40
  95.1 9.1 %copy-start.20 = (bf16[1024,2,64]{0,2,1:T(8,128)(2,1)S(1)}, bf16[1024,2,64]{0,2,1:T(8,128)(2,1)}, u32[]{:S(2)}) copy-start(bf16[1024,2,64]{0,2,1:T(8,128)(2,1)} %param.24) | copy-start | bytes 786436
  104.3 11.2 %copy-start.2 = (bf16[8,2,576,576]{2,3,1,0:T(8,128)(2,1)}, bf16[8,2,576,576]{2,3,1,0:T(8,128)(2,1)S(1)}, u32[]{:S(2)}) copy-start(bf16[8,2,576,576]{2,3,1,0:T(8,128)(2,1)S(1)} %divide_convert_fusion) | copy-start | bytes 31850500
  115.5 3.3 copy-start.14
  126.6 153.9 %all-gather.7.cloned.1.call-start = ((), (), s32[]{:S(2)}) async-start(), calls=%async_computation.6 | async-start | bytes 10616832 | tf_op jit(solution)/shard_map/all_gather | solution.py:48
  127.3 100.2 %copy-start.24 = (f32[1024]{0:T(1024)S(1)}, f32[1024]{0:T(1024)}, u32[]{:S(2)}) copy-start(f32[1024]{0:T(1024)} %param.28) | copy-start | bytes 12292
  127.3 100.2 %copy-start.36 = (f32[1024]{0:T(1024)S(1)}, f32[1024]{0:T(1024)}, u32[]{:S(2)}) copy-start(f32[1024]{0:T(1024)} %param.29) | copy-start | bytes 12292
  227.5 2.3 copy-start.39
  227.5 53.1 %copy-start.41 = (bf16[1024,512]{1,0:T(8,128)(2,1)S(1)}, bf16[1024,512]{1,0:T(8,128)(2,1)}, u32[]{:S(2)}) copy-start(bf16[1024,512]{1,0:T(8,128)(2,1)} %param.30) | copy-start | bytes 3145732
  229.1 104.1 %all-gather.9.cloned.1.call-start = ((), (), s32[]{:S(2)}) async-start(), calls=%async_computation.8 | async-start | bytes 10616832 | tf_op jit(solution)/shard_map/all_gather | solution.py:48
  229.7 228.6 %reduce-scatter.9.cloned.1.call-start = ((), (), s32[]{:S(2)}) async-start(), calls=%async_computation.9 | async-start | bytes 21233664 | tf_op jit(solution)/shard_map/reduce_scatter | solution.py:51
  360.1 198.7 %reduce-scatter.7.cloned.1.call-start = ((), (), s32[]{:S(2)}) async-start(), calls=%async_computation.7 | async-start | bytes 21233664 | tf_op jit(solution)/shard_map/reduce_scatter | solution.py:51
  373.9 241.0 %all-gather.11.cloned.1.call-start = ((), (), s32[]{:S(2)}) async-start(), calls=%async_computation.10 | async-start | bytes 10616832 | tf_op jit(solution)/shard_map/all_gather | solution.py:48
  463.1 151.8 %copy-start.15 = (bf16[2,64,1024]{2,1,0:T(8,128)(2,1)S(1)}, bf16[2,64,1024]{2,1,0:T(8,128)(2,1)}, u32[]{:S(2)}) copy-start(bf16[2,64,1024]{2,1,0:T(8,128)(2,1)} %param.26) | copy-start | bytes 786436
  563.4 249.8 %reduce-scatter.11.cloned.1.call-start = ((), (), s32[]{:S(2)}) async-start(), calls=%async_computation.11 | async-start | bytes 21233664 | tf_op jit(solution)/shard_map/reduce_scatter | solution.py:51
  661.9 15.6 %copy-start.17 = (bf16[1024,2,64]{0,2,1:T(8,128)(2,1)S(1)}, bf16[1024,2,64]{0,2,1:T(8,128)(2,1)}, u32[]{:S(2)}) copy-start(bf16[1024,2,64]{0,2,1:T(8,128)(2,1)} %param.23) | copy-start | bytes 786436
  677.5 9.4 %copy-start.12 = (bf16[8,576,2,64]{1,3,2,0:T(8,128)(2,1)S(1)}, bf16[8,576,2,64]{1,3,2,0:T(8,128)(2,1)}, u32[]{:S(2)}) copy-start(bf16[8,576,2,64]{1,3,2,0:T(8,128)(2,1)} %get-tuple-element.44) | copy-start | bytes 3538948
  677.5 9.4 %copy-start.19 = (bf16[1024,2,64]{0,2,1:T(8,128)(2,1)S(1)}, bf16[1024,2,64]{0,2,1:T(8,128)(2,1)}, u32[]{:S(2)}) copy-start(bf16[1024,2,64]{0,2,1:T(8,128)(2,1)} %param.21) | copy-start | bytes 786436
  686.9 7.9 copy-start.21
  715.1 21.3 %slice-start = ((s8[9437184]{0:T(1024)(128)(4,1)}), s8[4194304]{0:T(1024)(128)(4,1)S(1)}, s32[]{:S(2)}) async-start(s8[9437184]{0:T(1024)(128)(4,1)} %bitcast.173), calls=%async_computation.12 | async-start | bytes 8388608
  715.1 23.5 %slice-start.3 = ((s8[9437184]{0:T(1024)(128)(4,1)}), s8[4194304]{0:T(1024)(128)(4,1)S(1)}, s32[]{:S(2)}) async-start(s8[9437184]{0:T(1024)(128)(4,1)} %bitcast.185), calls=%async_computation.15 | async-start | bytes 8388608
  725.2 11.2 %copy-start.6 = (bf16[8,576,2,64]{1,3,2,0:T(8,128)(2,1)S(1)}, bf16[8,576,2,64]{1,3,2,0:T(8,128)(2,1)}, u32[]{:S(2)}) copy-start(bf16[8,576,2,64]{1,3,2,0:T(8,128)(2,1)} %copy-done.5) | copy-start | bytes 3538948
  725.2 11.2 %slice-start.1 = ((s8[9437184]{0:T(1024)(128)(4,1)}), s8[4194304]{0:T(1024)(128)(4,1)S(1)}, s32[]{:S(2)}) async-start(s8[9437184]{0:T(1024)(128)(4,1)} %bitcast.173), calls=%async_computation.13 | async-start | bytes 8388608
  725.2 11.2 %slice-start.2 = ((s8[9437184]{0:T(1024)(128)(4,1)}), s8[1048576]{0:T(1024)(128)(4,1)S(1)}, s32[]{:S(2)}) async-start(s8[9437184]{0:T(1024)(128)(4,1)} %bitcast.173), calls=%async_computation.14 | async-start | bytes 2097152
  725.2 13.3 %slice-start.4 = ((s8[9437184]{0:T(1024)(128)(4,1)}), s8[4194304]{0:T(1024)(128)(4,1)S(1)}, s32[]{:S(2)}) async-start(s8[9437184]{0:T(1024)(128)(4,1)} %bitcast.185), calls=%async_computation.16 | async-start | bytes 8388608
  725.2 13.3 %slice-start.5 = ((s8[9437184]{0:T(1024)(128)(4,1)}), s8[1048576]{0:T(1024)(128)(4,1)S(1)}, s32[]{:S(2)}) async-start(s8[9437184]{0:T(1024)(128)(4,1)} %bitcast.185), calls=%async_computation.17 | async-start | bytes 2097152
  743.0 70.2 %copy-start.4 = (bf16[8,72,1024]{2,1,0:T(8,128)(2,1)S(1)}, bf16[8,72,1024]{2,1,0:T(8,128)(2,1)}, u32[]{:S(2)}) copy-start(bf16[8,72,1024]{2,1,0:T(8,128)(2,1)} %param.17) | copy-start | bytes 3538948
  743.0 70.2 %copy-start.23 = (f32[8,72]{1,0:T(8,128)S(1)}, f32[8,72]{1,0:T(8,128)}, u32[]{:S(2)}) copy-start(f32[8,72]{1,0:T(8,128)} %copy-done.22) | copy-start | bytes 6916
  743.0 70.2 %copy-start.26 = (f32[1024]{0:T(1024)S(1)}, f32[1024]{0:T(1024)}, u32[]{:S(2)}) copy-start(f32[1024]{0:T(1024)} %param.19) | copy-start | bytes 12292
  745.2 70.4 %copy-start.30 = (f32[8,72]{1,0:T(8,128)S(1)}, f32[8,72]{1,0:T(8,128)}, u32[]{:S(2)}) copy-start(f32[8,72]{1,0:T(8,128)} %copy-done.29) | copy-start | bytes 6916
  745.2 71.4 %copy-start.28 = (f32[8,72]{1,0:T(8,128)S(1)}, f32[8,72]{1,0:T(8,128)}, u32[]{:S(2)}) copy-start(f32[8,72]{1,0:T(8,128)} %copy-done.27) | copy-start | bytes 6916
  815.5 2.5 copy-start.31
  815.6 2.5 copy-start.32
  815.6 2.5 copy-start.33
  815.6 2.5 copy-start.34
  815.6 24.5 %copy-start.7 = (bf16[8,72,1024]{2,1,0:T(8,128)(2,1)S(1)}, bf16[8,72,1024]{2,1,0:T(8,128)(2,1)}, u32[]{:S(2)}) copy-start(bf16[8,72,1024]{2,1,0:T(8,128)(2,1)} %get-tuple-element.28) | copy-start | bytes 3538948
  840.1 4.0 copy-start.1
  (11 other events, 14.5 us)
Sparse Core Ops, SparseCore 0:
  13.7 55.4 all-gather.4
  126.8 98.0 reduce-scatter.4
  229.2 51.3 all-gather.6
  282.0 51.1 all-gather.8
  360.2 98.0 reduce-scatter.8
  460.5 98.2 reduce-scatter.6
  563.5 51.3 all-gather.10
  715.2 97.9 reduce-scatter.10
where the time goes:
time: 858 us; the launch traced here: 851 us
  waiting for transfers between devices  546 us (64%)
  matrix products  225 us (26%)
  other arithmetic  34.8 us (4%)
  blocking collectives  21.3 us (2%)
  between operations  14.9 us (2%)
  local copies, waits for them, and re-layouts  8.94 us (1%)
    reduce_scatter x4, waiting for transfers between devices, scatter_sum(): return lax.psum_scatter(part_sum, 'tp', scatter_dimension=1, tiled=True)  345 us
    all_gather x4, waiting for transfers between devices, gather_tokens(): return lax.all_gather(local_rows, 'tp', axis=1, tiled=True)  200 us
    dot_general x2, matrix products, attention_core(): jnp.einsum('bqhd,bkhd->bhqk', queries, keys, preferred_element_type=jnp.f...  30.6 us
    dot_general x3, matrix products, attention_core(): jnp.einsum('bhqk,bkhd->bqhd', probs, values, preferred_element_type=jnp.f...  26.1 us
    psum x1, blocking collectives, layer_step(): lax.psum(jnp.stack([g_ln1_gain, g_ln1_bias, token_sum(d_mid), g_ln2_gain,...  21.3 us
    dot_general x1, matrix products, layer_step(): jnp.einsum('bnhd,whd->bnw', d_value, w_v, preferred_element_type=jnp.floa...  20.2 us
  transfers between devices with their start and end apart: 8, of which 8 were waited for; matrix products, arithmetic and copies ran while one was open for 7% of the time, Pallas kernels for 0%

commit v1 on v0

v1 whole, which is shorter than its diff:
```python
import math
import jax
import jax.numpy as jnp
from jax import lax
from jax.sharding import PartitionSpec as P

LN_EPS = 1e-6
F32 = jnp.float32
BF16 = jnp.bfloat16


def layer_norm(rows, ln_gain, ln_bias):
    row_mean = jnp.mean(rows, axis=-1, keepdims=True)
    centered = rows - row_mean
    variance = jnp.mean(centered * centered, axis=-1, keepdims=True)
    return centered * lax.rsqrt(variance + LN_EPS) * ln_gain + ln_bias


def gelu_tanh(pre_act):
    return jax.nn.gelu(pre_act, approximate=True)


def dot(eq, a, b):
    return jnp.einsum(eq, a, b, preferred_element_type=F32)


def attention_core(qkv):
    g, n, f = qkv.shape
    hd = 64
    h = f // (3 * hd)
    parts = qkv.reshape(g, n, 3, h, hd)
    queries, keys, values = parts[:, :, 0], parts[:, :, 1], parts[:, :, 2]
    att_scale = 1.0 / math.sqrt(hd)
    scores = dot('gqhd,gkhd->ghqk', queries, keys) * att_scale
    probs = jax.nn.softmax(scores, axis=-1).astype(BF16)
    mixed = dot('ghqk,gkhd->gqhd', probs, values)
    return mixed.astype(BF16).reshape(g, n, h * hd)


def solution(mesh):
    act_spec = P('dp', 'tp', None)
    replicated = P()
    head_w = P(None, 'tp', None)
    head_b = P('tp', None)
    grad_head_w = P('dp', 'tp', None)
    grad_head_b = P(('dp', 'tp'), None)
    grad_vec = P('dp')
    in_specs = (act_spec, act_spec, replicated, replicated, head_w, head_b, head_w, head_w, head_b,
                P('tp', None, None), replicated, replicated, replicated, P(None, 'tp'), P('tp'), P('tp', None), replicated)
    out_specs = (act_spec, act_spec, grad_vec, grad_vec, grad_head_w, grad_head_b, grad_head_w, grad_head_w, grad_head_b,
                 P(('dp', 'tp'), None, None), grad_vec, grad_vec, grad_vec, P('dp', 'tp'), P(('dp', 'tp')),
                 P(('dp', 'tp'), None), grad_vec)

    def gather(a):
        return lax.all_gather(a, 'tp', axis=0, tiled=False)

    def to_image(a):
        return lax.all_to_all(a, 'tp', split_axis=0, concat_axis=1, tiled=True)

    def to_tokens(a):
        return lax.all_to_all(a, 'tp', split_axis=1, concat_axis=0, tiled=True)

    def layer_step(x, d_out, ln1_gain, ln1_bias, w_q, b_q, w_k, w_v, b_v, w_o, b_o, ln2_gain, ln2_bias, w_1, b_1, w_2, b_2):
        width = x.shape[-1]
        heads_loc, hd = w_q.shape[1:]
        hw = heads_loc * hd
        wqkv_loc = jnp.concatenate([w.reshape(width, hw) for w in (w_q, w_k, w_v)], axis=1)
        bqkv_loc = jnp.concatenate([b_q.reshape(hw), jnp.zeros((hw,), b_q.dtype), b_v.reshape(hw)])
        wqkv = gather(wqkv_loc)
        bqkv = gather(bqkv_loc)
        wo = gather(w_o.reshape(hw, width))
        w1 = gather(w_1)
        b1 = gather(b_1)
        w2 = gather(w_2)
        d_out_all = lax.all_gather(d_out, 'tp', axis=1, tiled=True)
        me = lax.axis_index('tp')

        xi = to_image(x)[0]
        x_f32 = xi.astype(F32)
        h_one_f, ln1_pull = jax.vjp(layer_norm, x_f32, ln1_gain, ln1_bias)
        h_one = h_one_f.astype(BF16)
        qkv = (dot('nw,dwf->dnf', h_one, wqkv) + bqkv[:, None, :]).astype(BF16)
        mixed, attn_pull = jax.vjp(attention_core, qkv)
        attn_out = dot('dnf,dfw->nw', mixed, wo)
        x_mid = (x_f32 + attn_out + b_o).astype(BF16)
        mid_f32 = x_mid.astype(F32)
        h_two_f, ln2_pull = jax.vjp(layer_norm, mid_f32, ln2_gain, ln2_bias)
        h_two = h_two_f.astype(BF16)
        h_two_all = gather(h_two)
        pre_act = (dot('nw,dwf->dnf', h_two, w1) + b1[:, None, :]).astype(BF16)
        hidden_f, gelu_pull = jax.vjp(gelu_tanh, pre_act.astype(F32))
        hidden = hidden_f.astype(BF16)
        mlp_out = dot('dnf,dfw->nw', hidden, w2)
        y_img = (mid_f32 + mlp_out + b_2).astype(BF16)
        y_out = to_tokens(y_img[None])

        d_img = lax.dynamic_index_in_dim(d_out_all, me, 0, keepdims=False)
        d_hidden = dot('nw,dfw->dnf', d_img, w2).astype(BF16)
        (d_pre_f,) = gelu_pull(d_hidden.astype(F32))
        d_pre = d_pre_f.astype(BF16)
        d_h_two = dot('dnf,dwf->nw', d_pre, w1).astype(BF16)
        d_mid_ln, g_ln2_gain, g_ln2_bias = ln2_pull(d_h_two.astype(F32))
        d_mid = (d_img.astype(F32) + d_mid_ln).astype(BF16)
        d_mixed = dot('nw,dfw->dnf', d_mid, wo).astype(BF16)
        g_wo_part = dot('dnf,nw->dfw', mixed, d_mid)
        grad_w_o = lax.psum_scatter(g_wo_part, 'tp', scatter_dimension=0).astype(BF16).reshape(w_o.shape)
        (d_qkv,) = attn_pull(d_mixed)
        g_qkv_part = dot('nw,dnf->dwf', h_one, d_qkv)
        g_qkv = lax.psum_scatter(g_qkv_part, 'tp', scatter_dimension=0).astype(BF16)
        d_h_one = dot('dnf,dwf->nw', d_qkv, wqkv).astype(BF16)
        d_in_ln, g_ln1_gain, g_ln1_bias = ln1_pull(d_h_one.astype(F32))
        gx_img = (d_mid.astype(F32) + d_in_ln).astype(BF16)
        grad_x = to_tokens(gx_img[None])

        u_loc = (dot('bnw,wf->bnf', h_two_all, w_1) + b_1).astype(BF16)
        g_loc_f, gelu_pull2 = jax.vjp(gelu_tanh, u_loc.astype(F32))
        g_loc = g_loc_f.astype(BF16)
        dh_loc = dot('bnw,fw->bnf', d_out_all, w_2).astype(BF16)
        (dp_f,) = gelu_pull2(dh_loc.astype(F32))
        dp = dp_f.astype(BF16)
        grad_b_1 = jnp.sum(dp, axis=(0, 1), dtype=F32).astype(BF16)
        grad_w_1 = dot('bnw,bnf->wf', h_two_all, dp).astype(BF16)
        grad_w_2 = dot('bnf,bnw->fw', g_loc, d_out_all).astype(BF16)

        g_b_part = jnp.sum(d_qkv, axis=1, dtype=F32).reshape(-1, width)
        vec = jnp.concatenate([jnp.stack([g_ln1_gain, g_ln1_bias, g_ln2_gain, g_ln2_bias,
                                          jnp.sum(d_mid, axis=0, dtype=F32), jnp.sum(d_img, axis=0, dtype=F32)]), g_b_part])
        vec = lax.psum(vec, 'tp')
        gb = lax.dynamic_index_in_dim(vec[6:].reshape(-1, 3 * hw), me, 0, keepdims=False)
        grad_b_q = gb[:hw].astype(BF16).reshape(b_q.shape)
        grad_b_v = gb[2 * hw:].astype(BF16).reshape(b_v.shape)
        gq, gk, gv = (g_qkv[:, i * hw:(i + 1) * hw].reshape(w_q.shape) for i in range(3))
        return (y_out, grad_x, vec[0], vec[1], gq, grad_b_q, gk, gv, grad_b_v, grad_w_o,
                vec[4].astype(BF16), vec[2], vec[3], grad_w_1, grad_b_1, grad_w_2, vec[5].astype(BF16))

    return jax.shard_map(layer_step, mesh=mesh, in_specs=in_specs, out_specs=out_specs, check_vma=False)
```

time: 858 us -> 504 us (0.59)
  waiting for transfers between devices: 546 us -> 113 us
  blocking collectives: 21.3 us -> 76.8 us
  matrix products: 225 us -> 188 us
  local copies, waits for them, and re-layouts: 8.94 us -> 42.4 us
  starting transfers between devices: 0.51 us -> 15.9 us
  other arithmetic: 34.8 us -> 47.9 us
    reduce_scatter x4 -> x2, waiting for transfers between devices: 345 us -> 0.01 us  [the longest x1 0.01 us: layer_step(): lax.psum_scatter(g_wo_part, 'tp', scatter_dimension=0).astype(BF16)]
    all_gather x4 -> x6, waiting for transfers between devices: 200 us -> 110 us  [the longest x5 57.2 us: gather(): return lax.all_gather(a, 'tp', axis=0, tiled=False)]
    all_gather x0 -> x2, blocking collectives: none -> 45.9 us  [gather(): return lax.all_gather(a, 'tp', axis=0, tiled=False)]
    dot_general x23 -> x18, matrix products: 211 us -> 175 us  [dot(): return jnp.einsum(eq, a, b, preferred_element_type=F32)]
    unnamed x2 -> x4, other arithmetic: 0.01 us -> 16.3 us
    all_to_all x0 -> x3, starting transfers between devices: none -> 15.5 us  [the longest x2 9.45 us: to_tokens(): return lax.all_to_all(a, 'tp', split_axis=1, concat_axis=0, tiled=True)]
    unnamed x102 -> x93, local copies, waits for them, and re-layouts: 7.67 us -> 21.7 us
    convert_element_type x0 -> x4, local copies, waits for them, and re-layouts: none -> 9.73 us  [the longest x1 5.98 us: layer_step(): qkv = (dot('nw,dwf->dnf', h_one, wqkv) + bqkv[:, None, :]).astype(BF16)]
  transfers between devices with their start and end apart: 8 -> 11, of which waited for: 8 -> 3; matrix products, arithmetic and copies ran while one was open for 7% -> 47% of each run, Pallas kernels for 0% -> 0%
where the time goes in v1:
time: 504 us; the launch traced here: 499 us
  matrix products  188 us (37%)
  waiting for transfers between devices  113 us (22%)
  blocking collectives  76.8 us (15%)
  other arithmetic  47.9 us (10%)
  local copies, waits for them, and re-layouts  42.4 us (8%)
  starting transfers between devices  15.9 us (3%)
  between operations  14.9 us (3%)
    dot_general x18, matrix products, dot(): return jnp.einsum(eq, a, b, preferred_element_type=F32)  175 us
    all_gather x5, waiting for transfers between devices, gather(): return lax.all_gather(a, 'tp', axis=0, tiled=False)  57.2 us
    all_gather x1, waiting for transfers between devices, layer_step(): d_out_all = lax.all_gather(d_out, 'tp', axis=1, tiled=True)  52.6 us
    all_gather x2, blocking collectives, gather(): return lax.all_gather(a, 'tp', axis=0, tiled=False)  45.9 us
    psum x1, blocking collectives, layer_step(): vec = lax.psum(vec, 'tp')  30.9 us
    unnamed x93, local copies, waits for them, and re-layouts  21.7 us
    unnamed x4, other arithmetic  16.3 us
    sub x1, matrix products, attention_core(): probs = jax.nn.softmax(scores, axis=-1).astype(BF16)  13 us
  transfers between devices with their start and end apart: 11, of which 3 were waited for; matrix products, arithmetic and copies ran while one was open for 47% of the time, Pallas kernels for 0%

profile of v1, /device:TPU:81, one launch (start us, length us, event | category | flops | bytes accessed | tf_op | source)
XLA Modules:
  0.0 498.8 jit_solution(231641382031397277)
XLA Ops:
  14.6 6.0 %all-to-all-start = ((bf16[8,72,1024]{2,1,0:T(8,128)(2,1)}), bf16[8,72,1024]{2,1,0:T(8,128)(2,1)S(1)}, u32[]{:S(2)}, u32[]{:S(2)}) async-start(bf16[8,72,1024]{2,1,0:T(8,128)(2,1)} %param.17), calls=%async_computation | async-start | bytes 2359296 | tf_op jit(solution)/shard_map/all_to_all | solution.py:58
  20.7 33.0 %all-gather.7 = bf16[8,1,512]{2,1,0:T(2,128)(2,1)S(1)} all-gather(bf16[1,1,512]{2,1,0:T(2,128)(2,1)S(1)} %reshape.282), channel_id=5, replica_groups=mesh['dp'=4,'tp'=8] {'tp'}, dimensions={0}, use_global_device_ids=true | all-gather | bytes 9216 | tf_op jit(solution)/shard_map/all_gather | solution.py:55
  54.5 12.9 %all-gather.6 = bf16[8,1,384]{2,1,0:T(2,128)(2,1)S(1)} all-gather(bf16[1,1,384]{2,1,0:T(2,128)(2,1)S(1)} %reshape.280), channel_id=3, replica_groups=mesh['dp'=4,'tp'=8] {'tp'}, dimensions={0}, use_global_device_ids=true | all-gather | bytes 6912 | tf_op jit(solution)/shard_map/all_gather | solution.py:55
  69.0 8.6 %fusion.40 = bf16[8,576,384]{2,1,0:T(8,128)(2,1)} fusion(f32[8,384]{1,0:T(8,128)S(1)} %bitcast.263, bf16[8,1024,384]{2,1,0:T(8,128)(2,1)} %bitcast.279, f32[1024]{0:T(1024)S(1)} %copy-done.25, f32[1024]{0:T(1024)S(1)} %copy-done.15, f32[576]{0:T(1024)S(1)} %rsqrt.23, f32[576]{0:T(1024)S(1)} %div.61, bf16[576,1024]{1,0:T(8,128)(2,1)S(1)} %bitcast.229), kind=kOutput, calls=%fused_computation.57 | convolution fusion | flops 3630956544 | bytes 11035136 | tf_op jit(solution)/shard_map/nw,dwf->dnf/dot_general | solution.py:24
  77.6 6.0 %copy.86 = bf16[8,576,384]{1,2,0:T(8,128)(2,1)} copy(bf16[8,576,384]{2,1,0:T(8,128)(2,1)} %fusion.40) | data formatting | bytes 7077888 | tf_op jit(solution)/shard_map/convert_element_type | solution.py:82
  83.6 13.0 %fusion.116 = (f32[8,2,576]{2,1,0:T(2,128)S(1)}, f32[8,2,576,576]{2,3,1,0:T(8,128)}) fusion(bf16[8,576,3,2,64]{1,4,3,2,0:T(8,128)(2,1)} %bitcast.233), kind=kOutput, calls=%fused_computation.172 | convolution fusion | flops 695403072 | bytes 23891968 | tf_op jit(solution)/shard_map/jvp()/sub | solution.py:35
  96.6 9.1 %divide_convert_fusion = bf16[8,2,576,576]{2,3,1,0:T(8,128)(2,1)S(1)} fusion(f32[8,2,576,576]{2,3,1,0:T(8,128)} %get-tuple-element.43, f32[8,2,576]{2,1,0:T(2,128)S(1)} %get-tuple-element.42), kind=kLoop, calls=%fused_computation.8 | loop fusion | flops 10616832 | bytes 31887360 | tf_op jit(solution)/shard_map/jvp()/convert_element_type | solution.py:35
  105.7 4.3 copy-done
  110.0 4.6 convolution_convert_fusion.4
  114.6 3.4 fusion.61
  119.3 19.0 %all-gather.21.cloned.1.call-done = bf16[8192,512]{1,0:T(8,128)(2,1)} async-done(((bf16[1024,512]{1,0:T(8,128)(2,1)}), bf16[8192,512]{1,0:T(8,128)(2,1)}) %all-gather.21.cloned.1.call-update) | async-done | bytes 8388624 | tf_op jit(solution)/shard_map/all_gather | solution.py:55
  138.3 10.0 %add_convert_fusion.1 = bf16[576,8,512]{2,0,1:T(8,128)(2,1)} fusion(f32[8,512]{1,0:T(8,128)} %bitcast.260, bf16[8,1024,512]{2,1,0:T(8,128)(2,1)} %bitcast.277, bf16[576,1024]{1,0:T(8,128)(2,1)S(1)} %fusion.50), kind=kOutput, calls=%fused_computation.48 | convolution fusion | flops 4836556800 | bytes 14303232 | tf_op jit(solution)/shard_map/nw,dwf->dnf/dot_general | solution.py:24
  148.3 38.2 %all-gather.23.cloned.1.call-done = bf16[4096,1024]{1,0:T(8,128)(2,1)} async-done(((bf16[512,1024]{1,0:T(8,128)(2,1)}), bf16[4096,1024]{1,0:T(8,128)(2,1)}) %all-gather.23.cloned.1.call-update) | async-done | bytes 8388624 | tf_op jit(solution)/shard_map/all_gather | solution.py:55
  186.5 52.6 %all-gather.17.cloned.1.call-done = bf16[8,576,1024]{2,1,0:T(8,128)(2,1)} async-done(((bf16[8,72,1024]{2,1,0:T(8,128)(2,1)}), bf16[8,576,1024]{2,1,0:T(8,128)(2,1)}) %all-gather.17.cloned.1.call-update) | async-done | bytes 9437200 | tf_op jit(solution)/shard_map/all_gather | solution.py:75
  239.0 18.7 %convert_reduce_fusion.2 = (f32[1024]{0:T(1024)}, f32[576]{0:T(1024)}, bf16[576,1024]{1,0:T(8,128)(2,1)S(1)}) fusion(f32[1024]{0:T(1024)} %param.28, f32[576]{0:T(1024)S(1)} %broadcast_multiply_fusion, bf16[576,1024]{1,0:T(8,128)(2,1)S(1)} %fusion.61, bf16[8,1024,512]{2,1,0:T(8,128)(2,1)} %bitcast.278, bf16[576,8,512]{2,0,1:T(8,128)(2,1)} %add_convert_fusion.1, ...), kind=kOutput, calls=%fused_computation.63 | convolution fusion | flops 9720297472 | bytes 25047556 | tf_op jit(solution)/shard_map/dnf,dwf->nw/dot_general | solution.py:24
  258.4 2.1 fusion.58
  260.6 3.0 convert_reduce_fusion.4
  264.5 3.8 fusion.79
  269.3 2.2 add_convert_fusion.3
  273.0 4.0 fusion.75
  277.0 2.6 copy.93
  279.5 15.0 %fusion.5 = (f32[8,2,576]{2,1,0:T(2,128)S(1)}, bf16[8,2,576,576]{2,3,1,0:T(8,128)(2,1)}) fusion(f32[8,2,576,576]{2,3,1,0:T(8,128)} %get-tuple-element.43, f32[8,2,576]{2,1,0:T(2,128)} %multiply_divide_fusion, bf16[8,2,64,576]{3,2,1,0:T(8,128)(2,1)} %bitcast.231, bf16[8,576,3,2,64]{1,4,3,2,0:T(8,128)(2,1)} %bitcast.235), kind=kOutput, calls=%fused_computation.7 | convolution fusion | flops 706010112 | bytes 36909056 | tf_op jit(solution)/shard_map/transpose(jvp(ghqk,gkhd->gqhd))/dot_general | solution.py:24
  294.6 9.4 %fusion.69 = bf16[8,576,1,2,64]{1,4,3,0,2:T(8,128)(2,1)} fusion(bf16[8,2,64,576]{3,2,1,0:T(8,128)(2,1)} %bitcast.232, bf16[8,2,576,576]{2,3,1,0:T(8,128)(2,1)} %copy-done), kind=kOutput, calls=%fused_computation.109 | convolution fusion | flops 680067072 | bytes 12976128 | tf_op jit(solution)/shard_map/transpose(jvp(ghqk,gkhd->gqhd))/dot_general | solution.py:24
  304.0 15.0 %fusion.71 = bf16[8,576,1,2,64]{1,4,3,0,2:T(8,128)(2,1)} fusion(bf16[8,576,3,2,64]{1,4,3,2,0:T(8,128)(2,1)} %bitcast.236, f32[8,2,576,576]{2,3,1,0:T(8,128)} %get-tuple-element.43, bf16[8,2,576,576]{2,3,1,0:T(8,128)(2,1)} %get-tuple-element.46, f32[8,2,576]{2,1,0:T(2,128)S(1)} %neg.13, f32[8,2,576]{2,1,0:T(2,128)S(1)} %copy-done.10), kind=kOutput, calls=%fused_computation.111 | convolution fusion | flops 706609152 | bytes 37953536 | tf_op jit(solution)/shard_map/transpose(jvp(gqhd,gkhd->ghqk))/dot_general | solution.py:24
  319.0 15.0 %fusion.70 = bf16[8,576,1,2,64]{1,4,3,0,2:T(8,128)(2,1)} fusion(bf16[8,576,3,2,64]{1,4,3,2,0:T(8,128)(2,1)} %bitcast.237, f32[8,2,576,576]{2,3,1,0:T(8,128)} %get-tuple-element.43, bf16[8,2,576,576]{2,3,1,0:T(8,128)(2,1)} %get-tuple-element.46, f32[8,2,576]{2,1,0:T(2,128)S(1)} %neg.13, f32[8,2,576]{2,1,0:T(2,128)S(1)} %copy-done.10), kind=kOutput, calls=%fused_computation.110 | convolution fusion | flops 706609152 | bytes 37953536 | tf_op jit(solution)/shard_map/transpose(jvp(gqhd,gkhd->ghqk))/dot_general | solution.py:24
  334.0 3.1 convert_reduce_fusion
  337.6 1.8 copy-done.4
  339.5 8.3 %convolution_bitcast_fusion = f32[8,1024,384]{1,2,0:T(8,128)} fusion(bf16[8,576,384]{1,2,0:T(8,128)(2,1)S(1)} %bitcast.242, bf16[576,1024,1]{1,0,2:T(8,128)(2,1)S(1)} %bitcast.248), kind=kOutput, calls=%fused_computation.55 | convolution fusion | flops 3623878656 | bytes 17301504 | tf_op jit(solution)/shard_map/nw,dnf->dwf/dot_general | solution.py:24
  348.4 10.5 %fusion.72 = bf16[1,576,1024]{2,1,0:T(8,128)(2,1)S(1)} fusion(bf16[8,512,1024]{2,1,0:T(8,128)(2,1)} %bitcast.276, bf16[576,8,512]{2,0,1:T(8,128)(2,1)} %add_convert_fusion.1, bf16[576,1024]{1,0:T(8,128)(2,1)S(1)} %fusion.61, f32[1024]{0:T(1024)S(1)} %convert_element_type.228), kind=kOutput, calls=%fused_computation.112 | convolution fusion | flops 4857790464 | bytes 15470592 | tf_op jit(solution)/shard_map/dnf,dfw->nw/dot_general | solution.py:24
  358.9 1.8 copy.125
  361.3 8.6 %reduce.22 = bf16[576,1024]{1,0:T(8,128)(2,1)} reduce(bf16[576,1,1024]{2,1,0:T(2,128)(2,1)S(1)} %bitcast.238, bf16[]{:T(256)} %broadcast.277), dimensions={1}, to_apply=%bitcast.228.reduce_sub_computation | reduce | bytes 2359298
  369.8 2.6 reshape.315
  372.5 4.6 all-to-all-start.1
  377.1 9.7 %fusion.59 = (f32[1024]{0:T(1024)}, f32[576]{0:T(1024)S(1)}, f32[1024]{0:T(1024)}, bf16[576,1024]{1,0:T(8,128)(2,1)S(1)}) fusion(f32[576]{0:T(1024)S(1)} %copy-done.21, f32[576]{0:T(1024)S(1)} %copy-done.19, bf16[8,72,1024]{2,1,0:T(8,128)(2,1)S(1)} %all-to-all-done, f32[1024]{0:T(1024)S(1)} %copy-done.16, bf16[8,576,384]{1,2,0:T(8,128)(2,1)} %bitcast.243, ...), kind=kOutput, calls=%fused_computation.91 | convolution fusion | flops 3631543808 | bytes 13388544 | tf_op jit(solution)/shard_map/dnf,dwf->nw/dot_general | solution.py:24
  387.6 1.6 fusion.78
  389.3 1.8 copy.124
  391.1 7.8 %reduce.23 = bf16[576,1024]{1,0:T(8,128)(2,1)S(1)} reduce(bf16[576,1,1024]{2,1,0:T(2,128)(2,1)S(1)} %bitcast.239, bf16[]{:T(256)} %broadcast.277), dimensions={1}, to_apply=%bitcast.227.reduce_sub_computation | reduce | bytes 2359298
  398.9 1.6 reshape.317
  400.5 4.9 all-to-all-start.2
  405.9 4.4 reshape.316
  410.4 1.4 copy.113
  412.8 30.9 %psum.7 = f32[9,1024]{1,0:T(8,128)S(1)} all-reduce(f32[9,1024]{1,0:T(8,128)S(1)} %concatenate.11), channel_id=1, replica_groups=mesh['dp'=4,'tp'=8] {'tp'}, use_global_device_ids=true, to_apply=%region_18.19 | all-reduce | flops 9216 | bytes 73728 | tf_op jit(solution)/shard_map/psum | solution.py:128
  448.8 1.8 convert_element_type.259
  450.7 10.5 %add_convert_fusion = bf16[8,576,512]{2,1,0:T(8,128)(2,1)} fusion(f32[512]{0:T(512)S(1)} %copy-done.31, bf16[8,576,1024]{2,1,0:T(8,128)(2,1)} %bitcast.271, bf16[1024,512]{1,0:T(8,128)(2,1)S(1)} %copy-done.7), kind=kOutput, calls=%fused_computation.47 | convolution fusion | flops 4836556800 | bytes 15206400 | tf_op jit(solution)/shard_map/bnw,wf->bnf/dot_general | solution.py:24
  461.2 15.8 %fusion.117 = (bf16[512]{0:T(512)(128)(2,1)}, bf16[8,576,512]{2,1,0:T(8,128)(2,1)S(1)}) fusion(bf16[8,576,512]{2,1,0:T(8,128)(2,1)} %add_convert_fusion, bf16[8,576,1024]{2,1,0:T(8,128)(2,1)} %all-gather.17.cloned.1.call-done, bf16[512,1024]{1,0:T(8,128)(2,1)S(1)} %copy-done.8), kind=kOutput, calls=%fused_computation.173 | convolution fusion | flops 4888460800 | bytes 19923968 | tf_op jit(solution)/shard_map/bnw,fw->bnf/dot_general | solution.py:24
  477.0 6.0 %bitcast_convert_fusion.3 = bf16[1024,512]{1,0:T(8,128)(2,1)} fusion(bf16[8,576,1024]{2,1,0:T(8,128)(2,1)S(1)} %bitcast.274, bf16[8,576,512]{2,1,0:T(8,128)(2,1)S(1)} %get-tuple-element.49), kind=kOutput, calls=%fused_computation.102 | convolution fusion | flops 4832362496 | bytes 15204352 | tf_op jit(solution)/shard_map/bnw,bnf->wf/dot_general | solution.py:24
  483.1 6.3 %bitcast_convert_fusion.2 = bf16[512,1024]{1,0:T(8,128)(2,1)} fusion(bf16[8,576,1024]{2,1,0:T(8,128)(2,1)S(1)} %bitcast.258, bf16[8,576,512]{2,1,0:T(8,128)(2,1)S(1)} %copy-done.34), kind=kOutput, calls=%fused_computation.101 | convolution fusion | flops 4855955456 | bytes 15204352 | tf_op jit(solution)/shard_map/bnf,bnw->fw/dot_general | solution.py:24
  489.4 1.5 convert_bitcast_fusion
  (158 shorter events, 25.1 us)
Async XLA Ops:
  7.2 61.8 %all-gather.19.cloned.1.call-start = ((), (), s32[]{:S(2)}) async-start(), calls=%async_computation.9 | async-start | bytes 7077888 | tf_op jit(solution)/shard_map/all_gather | solution.py:55
  11.6 9.0 %copy-start.26 = (bf16[512]{0:T(512)(128)(2,1)S(1)}, bf16[512]{0:T(512)(128)(2,1)}, u32[]{:S(2)}) copy-start(bf16[512]{0:T(512)(128)(2,1)} %param.31) | copy-start | bytes 3076
  11.6 42.6 %copy-start.32 = (bf16[2,64]{1,0:T(2,128)(2,1)S(1)}, bf16[2,64]{1,0:T(2,128)(2,1)}, u32[]{:S(2)}) copy-start(bf16[2,64]{1,0:T(2,128)(2,1)} %param.25) | copy-start | bytes 772
  11.6 42.7 %copy-start.33 = (bf16[2,64]{1,0:T(2,128)(2,1)S(1)}, bf16[2,64]{1,0:T(2,128)(2,1)}, u32[]{:S(2)}) copy-start(bf16[2,64]{1,0:T(2,128)(2,1)} %param.22) | copy-start | bytes 772
  11.6 55.8 %copy-start.29 = (bf16[1024]{0:T(1024)(128)(2,1)S(1)}, bf16[1024]{0:T(1024)(128)(2,1)}, u32[]{:S(2)}) copy-start(bf16[1024]{0:T(1024)(128)(2,1)} %param.27) | copy-start | bytes 6148
  11.7 102.9 %all-gather.15.cloned.1.call-start = ((), (), s32[]{:S(2)}) async-start(), calls=%async_computation.5 | async-start | bytes 2359296 | tf_op jit(solution)/shard_map/all_gather | solution.py:55
  12.5 125.8 %all-gather.21.cloned.1.call-start = ((), (), s32[]{:S(2)}) async-start(), calls=%async_computation.10 | async-start | bytes 9437184 | tf_op jit(solution)/shard_map/all_gather | solution.py:55
  13.3 55.7 %copy-start.15 = (f32[1024]{0:T(1024)S(1)}, f32[1024]{0:T(1024)}, u32[]{:S(2)}) copy-start(f32[1024]{0:T(1024)} %param.19) | copy-start | bytes 12292
  13.3 55.7 %copy-start.25 = (f32[1024]{0:T(1024)S(1)}, f32[1024]{0:T(1024)}, u32[]{:S(2)}) copy-start(f32[1024]{0:T(1024)} %param.20) | copy-start | bytes 12292
  13.3 173.1 %all-gather.23.cloned.1.call-start = ((), (), s32[]{:S(2)}) async-start(), calls=%async_computation.11 | async-start | bytes 9437184 | tf_op jit(solution)/shard_map/all_gather | solution.py:55
  14.0 225.0 %all-gather.17.cloned.1.call-start = ((), (), s32[]{:S(2)}) async-start(), calls=%async_computation.6 | async-start | bytes 10616832 | tf_op jit(solution)/shard_map/all_gather | solution.py:75
  14.6 52.8 %all-to-all-start = ((bf16[8,72,1024]{2,1,0:T(8,128)(2,1)}), bf16[8,72,1024]{2,1,0:T(8,128)(2,1)S(1)}, u32[]{:S(2)}, u32[]{:S(2)}) async-start(bf16[8,72,1024]{2,1,0:T(8,128)(2,1)} %param.17), calls=%async_computation | async-start | bytes 2359296 | tf_op jit(solution)/shard_map/all_to_all | solution.py:58
  20.7 428.2 %reduce-scatter.5.cloned.1.call-start = ((), (), s32[]{:S(2)}) async-start(), calls=%async_computation.8 | async-start | bytes 4718592 | tf_op jit(solution)/shard_map/reduce_scatter | solution.py:106
  67.8 9.8 %copy-start.18 = (f32[576]{0:T(1024)}, f32[576]{0:T(1024)S(1)}, u32[]{:S(2)}) copy-start(f32[576]{0:T(1024)S(1)} %div.61) | copy-start | bytes 6916
  68.9 8.7 %copy-start.12 = (f32[576]{0:T(1024)}, f32[576]{0:T(1024)S(1)}, u32[]{:S(2)}) copy-start(f32[576]{0:T(1024)S(1)} %add.133) | copy-start | bytes 6916
  68.9 8.7 %copy-start.20 = (f32[576]{0:T(1024)}, f32[576]{0:T(1024)S(1)}, u32[]{:S(2)}) copy-start(f32[576]{0:T(1024)S(1)} %rsqrt.23) | copy-start | bytes 6916
  96.6 9.1 %copy-start.9 = (f32[8,2,576]{2,1,0:T(2,128)}, f32[8,2,576]{2,1,0:T(2,128)S(1)}, u32[]{:S(2)}) copy-start(f32[8,2,576]{2,1,0:T(2,128)S(1)} %get-tuple-element.42) | copy-start | bytes 110596
  105.7 4.3 copy-start
  114.6 4.2 copy-start.14
  114.6 4.2 copy-start.24
  119.3 29.0 %copy-start.1 = (bf16[576,1024]{1,0:T(8,128)(2,1)}, bf16[576,1024]{1,0:T(8,128)(2,1)S(1)}, u32[]{:S(2)}) copy-start(bf16[576,1024]{1,0:T(8,128)(2,1)S(1)} %fusion.50) | copy-start | bytes 3538948
  258.4 6.1 %copy-start.5 = (bf16[8,2,64,576]{3,2,1,0:T(8,128)(2,1)S(1)}, bf16[8,2,64,576]{3,2,1,0:T(8,128)(2,1)}, u32[]{:S(2)}) copy-start(bf16[8,2,64,576]{3,2,1,0:T(8,128)(2,1)} %convolution_convert_fusion.4) | copy-start | bytes 3538948
  268.4 4.6 copy-start.3
  268.4 182.2 %all-gather.25.cloned.1.call-start = ((), (), s32[]{:S(2)}) async-start(), calls=%async_computation.12 | async-start | bytes 10616832 | tf_op jit(solution)/shard_map/all_gather | solution.py:55
  269.2 220.1 %reduce-scatter.3.cloned.1.call-start = ((), (), s32[]{:S(2)}) async-start(), calls=%async_computation.7 | async-start | bytes 14155776 | tf_op jit(solution)/shard_map/reduce_scatter | solution.py:109
  294.6 9.4 %copy-start.10 = (f32[8,2,576]{2,1,0:T(2,128)S(1)}, f32[8,2,576]{2,1,0:T(2,128)}, u32[]{:S(2)}) copy-start(f32[8,2,576]{2,1,0:T(2,128)} %copy-done.9) | copy-start | bytes 110596
  337.1 2.4 copy-start.6
  337.6 1.9 copy-start.4
  361.3 15.8 %copy-start.19 = (f32[576]{0:T(1024)S(1)}, f32[576]{0:T(1024)}, u32[]{:S(2)}) copy-start(f32[576]{0:T(1024)} %copy-done.18) | copy-start | bytes 6916
  361.3 15.8 %copy-start.21 = (f32[576]{0:T(1024)S(1)}, f32[576]{0:T(1024)}, u32[]{:S(2)}) copy-start(f32[576]{0:T(1024)} %copy-done.20) | copy-start | bytes 6916
  372.5 28.0 %all-to-all-start.1 = ((bf16[8,2,36864]{2,1,0:T(2,128)(2,1)}), bf16[8,2,36864]{2,1,0:T(2,128)(2,1)}, u32[]{:S(2)}, u32[]{:S(2)}) async-start(bf16[8,2,36864]{2,1,0:T(2,128)(2,1)} %reshape.315), calls=%async_computation.1 | async-start | bytes 2359296 | tf_op jit(solution)/shard_map/all_to_all | solution.py:61
  377.1 9.7 %copy-start.13 = (f32[576]{0:T(1024)S(1)}, f32[576]{0:T(1024)}, u32[]{:S(2)}) copy-start(f32[576]{0:T(1024)} %copy-done.12) | copy-start | bytes 6916
  391.1 14.3 %copy-start.27 = (bf16[512]{0:T(512)(128)(2,1)S(1)}, bf16[512]{0:T(512)(128)(2,1)}, u32[]{:S(2)}) copy-start(bf16[512]{0:T(512)(128)(2,1)} %param.31) | copy-start | bytes 3076
  400.5 45.8 %all-to-all-start.2 = ((bf16[8,2,36864]{2,1,0:T(2,128)(2,1)}), bf16[8,2,36864]{2,1,0:T(2,128)(2,1)S(1)}, u32[]{:S(2)}, u32[]{:S(2)}) async-start(bf16[8,2,36864]{2,1,0:T(2,128)(2,1)} %reshape.317), calls=%async_computation.2 | async-start | bytes 2359296 | tf_op jit(solution)/shard_map/all_to_all | solution.py:61
  405.9 6.0 %copy-start.22 = (f32[1024]{0:T(1024)S(1)}, f32[1024]{0:T(1024)}, u32[]{:S(2)}) copy-start(f32[1024]{0:T(1024)} %get-tuple-element.30) | copy-start | bytes 12292
  405.9 6.0 %copy-start.23 = (f32[1024]{0:T(1024)S(1)}, f32[1024]{0:T(1024)}, u32[]{:S(2)}) copy-start(f32[1024]{0:T(1024)} %get-tuple-element.32) | copy-start | bytes 12292
  405.9 6.0 %copy-start.28 = (f32[1024]{0:T(1024)S(1)}, f32[1024]{0:T(1024)}, u32[]{:S(2)}) copy-start(f32[1024]{0:T(1024)} %get-tuple-element.21) | copy-start | bytes 12292
  410.4 1.5 copy-start.11
  446.2 4.4 copy-start.31
  447.4 3.2 copy-start.7
  450.6 10.6 %copy-start.8 = (bf16[512,1024]{1,0:T(8,128)(2,1)S(1)}, bf16[512,1024]{1,0:T(8,128)(2,1)}, u32[]{:S(2)}) copy-start(bf16[512,1024]{1,0:T(8,128)(2,1)} %param.32) | copy-start | bytes 3145732
  450.6 26.4 %slice-start.3 = ((s8[9437184]{0:T(1024)(128)(4,1)}), s8[4194304]{0:T(1024)(128)(4,1)S(1)}, s32[]{:S(2)}) async-start(s8[9437184]{0:T(1024)(128)(4,1)} %bitcast.272), calls=%async_computation.16 | async-start | bytes 8388608
  450.7 26.4 %slice-start.4 = ((s8[9437184]{0:T(1024)(128)(4,1)}), s8[4194304]{0:T(1024)(128)(4,1)S(1)}, s32[]{:S(2)}) async-start(s8[9437184]{0:T(1024)(128)(4,1)} %bitcast.272), calls=%async_computation.17 | async-start | bytes 8388608
  450.7 32.4 %slice-start = ((s8[9437184]{0:T(1024)(128)(4,1)}), s8[4194304]{0:T(1024)(128)(4,1)S(1)}, s32[]{:S(2)}) async-start(s8[9437184]{0:T(1024)(128)(4,1)} %bitcast.257), calls=%async_computation.13 | async-start | bytes 8388608
  461.2 15.8 %slice-start.5 = ((s8[9437184]{0:T(1024)(128)(4,1)}), s8[1048576]{0:T(1024)(128)(4,1)S(1)}, s32[]{:S(2)}) async-start(s8[9437184]{0:T(1024)(128)(4,1)} %bitcast.272), calls=%async_computation.18 | async-start | bytes 2097152
  461.2 21.9 %slice-start.1 = ((s8[9437184]{0:T(1024)(128)(4,1)}), s8[4194304]{0:T(1024)(128)(4,1)S(1)}, s32[]{:S(2)}) async-start(s8[9437184]{0:T(1024)(128)(4,1)} %bitcast.257), calls=%async_computation.14 | async-start | bytes 8388608
  461.2 21.9 %slice-start.2 = ((s8[9437184]{0:T(1024)(128)(4,1)}), s8[1048576]{0:T(1024)(128)(4,1)S(1)}, s32[]{:S(2)}) async-start(s8[9437184]{0:T(1024)(128)(4,1)} %bitcast.257), calls=%async_computation.15 | async-start | bytes 2097152
  477.0 6.0 %copy-start.34 = (bf16[8,576,512]{2,1,0:T(8,128)(2,1)S(1)}, bf16[8,576,512]{2,1,0:T(8,128)(2,1)}, u32[]{:S(2)}) copy-start(bf16[8,576,512]{2,1,0:T(8,128)(2,1)} %add_convert_fusion) | copy-start | bytes 14155780
  (4 other events, 3.6 us)
Sparse Core Ops, SparseCore 0:
  11.8 52.5 all-gather.18
  66.0 23.5 all-gather.14
  91.2 47.0 all-gather.20
  139.8 46.6 all-gather.22
  187.9 51.0 all-gather.16
  268.6 31.8 reduce-scatter.4
  302.0 52.9 all-gather.24
  357.3 94.5 reduce-scatter.2

commit v2 on v0

v2 whole, which is shorter than its diff:
```python
import functools
import math
import jax
import jax.numpy as jnp
from jax import lax
from jax.experimental import pallas as pl
from jax.experimental.pallas import tpu as pltpu
from jax.sharding import PartitionSpec as P

LN_EPS = 1e-6
F32 = jnp.float32
BF16 = jnp.bfloat16
NN = (((1,), (0,)), ((), ()))
NT = (((1,), (1,)), ((), ()))
TN = (((0,), (0,)), ((), ()))
BIAS_ROWS = 16


def mm(a, b, dims):
    return lax.dot_general(a, b, dims, preferred_element_type=F32)


def push(src, dst, ssem, rsem, dev):
    return pltpu.make_async_remote_copy(src_ref=src, dst_ref=dst, send_sem=ssem, recv_sem=rsem,
                                        device_id={'tp': dev}, device_id_type=pl.DeviceIdType.MESH)


def greet_all(size):
    me = lax.axis_index('tp')
    barrier = pltpu.get_barrier_semaphore()
    for r in range(1, size):
        pl.semaphore_signal(barrier, inc=1, device_id={'tp': lax.rem(me + r, size)}, device_id_type=pl.DeviceIdType.MESH)
    pl.semaphore_wait(barrier, size - 1)


def swap_core(dev):
    return dev + 1 - 2 * lax.rem(dev, 2)


def ring(size):
    me = lax.axis_index('tp')
    return me, lax.rem(me + 2, size), lax.rem(me + size - 2, size), lax.rem(me + size // 2, size)


class Gather:
    COPIES = 14

    def __init__(self, size, src, dst, sems, off):
        me, right, left, opp = ring(size)
        partner = swap_core(me)
        plan = [(me, 0, right), (me, 1, right), (left, 0, right), (me, 1, left), (me, 0, left), (right, 1, left)]
        plan += [(owner, half, partner) for owner in (me, left, right, opp) for half in range(2)]

        def make(i):
            owner, half, dev = plan[i]
            out = dst(owner, half)
            return push(src(half) if owner is me else out, out, sems[0].at[off + i], sems[1].at[off + i], dev)

        self.copy = make

    def start(self):
        for i in (0, 3, 1, 4, 6, 7):
            self.copy(i).start()

    def forward(self):
        for got, sends in ((0, (2, 8)), (3, (5, 11))):
            self.copy(got).wait_recv()
            for i in sends:
                self.copy(i).start()

    def relay(self, *pairs):
        for got, i in pairs:
            self.copy(got).wait_recv()
            self.copy(i).start()

    def near(self):
        self.relay((1, 9), (4, 10))

    def far(self):
        self.relay((2, 12), (5, 13))

    def received(self, *which):
        for i in which:
            self.copy(i).wait_recv()

    def sent(self):
        for i in range(self.COPIES):
            self.copy(i).wait_send()

    def follow(self, step, after_forward):
        def at(k, *calls):
            @pl.when(step == k)
            def _():
                for call in calls:
                    call()

        at(1, lambda: self.received(6, 7))
        at(2, self.forward, after_forward, lambda: self.relay((1, 9)))
        at(3, lambda: self.relay((4, 10)))
        at(4, lambda: self.received(8, 9))
        at(5, lambda: self.received(10, 11))
        at(6, self.far)
        at(7, lambda: self.received(12, 13))


class Exchange:
    COPIES = 9

    def __init__(self, size, src, dst, via, sems, off):
        me, right, left, opp = ring(size)
        plan = [(src(opp), via.at[0], left), (src(swap_core(opp)), via.at[1], right)]
        plan += [(src(dev), dst(me), dev) for side in (right, left) for dev in (side, swap_core(side))]
        plan += [(src(swap_core(me)), dst(me), swap_core(me)), (via.at[0], dst(right), left), (via.at[1], dst(left), swap_core(right))]
        self.copy = lambda i: push(*plan[i][:2], sems[0].at[off + i], sems[1].at[off + i], plan[i][2])

    def start(self):
        for i in range(7):
            self.copy(i).start()

    def forward(self):
        for got, i in ((0, 7), (1, 8)):
            self.copy(got).wait_recv()
            self.copy(i).start()

    def close(self):
        for i in range(2, self.COPIES):
            self.copy(i).wait_recv()
        for i in range(self.COPIES):
            self.copy(i).wait_send()


def pair_rows(ref, c):
    return jnp.concatenate([ref[2 * c].astype(F32), ref[2 * c + 1].astype(F32)])


def pair_chunks(size, tok, body):
    pl.loop(0, size // 2)(lambda c: body(c, pl.ds(pl.multiple_of(c * 2 * tok, 16), 2 * tok)))


def cut(rows):
    half = rows // 2 // 16 * 16
    return pl.ds(0, half), pl.ds(half, rows - half)


def head(z, i, hd):
    return z[i * hd:(i + 1) * hd]


def norm_rows(z):
    centered = z - jnp.mean(z, axis=-1, keepdims=True)
    inv = lax.rsqrt(jnp.mean(centered * centered, axis=-1, keepdims=True) + LN_EPS)
    return centered * inv, inv


def norm_rows_pull(xhat, inv, dh, gain):
    dxh = dh * gain
    return inv * (dxh - jnp.mean(dxh, axis=-1, keepdims=True) - xhat * jnp.mean(dxh * xhat, axis=-1, keepdims=True))


def arrival(i, size):
    me = lax.axis_index('tp')
    partner = me + 1 - 2 * lax.rem(me, 2)
    hop = jnp.where(i < 2, 0, jnp.where(i >= 6, size // 2, jnp.where(lax.rem(i, 2) == 0, size - 2, 2)))
    base = jnp.where((i == 1) | (i == 4) | (i == 5) | (i == 7), partner, me)
    return lax.rem(base + hop, size)


def front_kernel(heads, hd, size, x_ref, wl_ref, g1_ref, c1_ref, bo_ref, g2_ref, c2_ref, w1_ref, do_ref,
                 qkv_ref, mix_ref, st_ref, h1_ref, xm_ref, h2_ref, xi_ref, wa_ref, doa_ref, w1a_ref,
                 w_all, x_all, via, acc_ref, own_do, loc_sem, out_sem, send_sem, recv_sem):
    hw = heads * hd
    scale = 1.0 / math.sqrt(hd)
    step = pl.program_id(0)
    me = lax.axis_index('tp')
    imgs, tok, width = x_ref.shape
    n = h1_ref.shape[0]
    rows = wl_ref.shape[0]
    sems = send_sem, recv_sem
    images = pl.ds(0, imgs // 2), pl.ds(imgs // 2, imgs // 2)
    mine = lambda dev: pl.ds(pl.multiple_of(dev * tok, 8), tok)
    gw = Gather(size, lambda h: wl_ref.at[cut(rows)[h]], lambda d, h: w_all.at[d, cut(rows)[h]], sems, 0)
    gw1 = Gather(size, lambda h: w1_ref.at[cut(width)[h]], lambda d, h: w1a_ref.at[d, cut(width)[h]], sems, Gather.COPIES)
    gdo = Gather(size, lambda h: do_ref.at[images[h]], lambda d, h: doa_ref.at[images[h], mine(d)], sems, 2 * Gather.COPIES)
    ex = Exchange(size, lambda d: x_ref.at[d], lambda d: x_all.at[d], via, sems, 3 * Gather.COPIES)
    local = lambda src, dst, i: pltpu.make_async_copy(src, dst, loc_sem.at[i])
    in_x, in_do = local(x_ref.at[me], x_all.at[me], 0), local(do_ref, own_do, 1)
    out_w, out_w1 = local(wl_ref, wa_ref.at[me], 2), local(w1_ref, w1a_ref.at[me], 3)
    out_x, out_do = local(x_all, xi_ref, 4), local(own_do, doa_ref.at[:, mine(me)], 5)

    def out_block(i):
        dev = arrival(i, size)
        return pltpu.make_async_copy(w_all.at[dev], wa_ref.at[dev], out_sem.at[i])

    @pl.when(step == 0)
    def _():
        for c in (in_x, in_do, out_w, out_w1):
            c.start()
        greet_all(size)
        ex.start()
        gw.start()
        w_all[me] = wl_ref[...]
        ex.forward()
        in_x.wait()
        ex.close()
        out_x.start()

        def body(c, rows):
            xhat, _ = norm_rows(pair_rows(x_all, c))
            h1_ref[rows] = (xhat * g1_ref[...] + c1_ref[...]).astype(BF16)

        pair_chunks(size, tok, body)
        in_do.wait()
        out_do.start()

    gw.follow(step, gw1.start)

    @pl.when(step > 0)
    def _():
        out_block(step).start()

    w = w_all.at[arrival(step, size)]
    bias = mm(w[4 * hw:, :3 * hw], jnp.ones((BIAS_ROWS, n), BF16), TN)
    qkv = (mm(w[:3 * hw], h1_ref[...], NT) + bias).astype(BF16)
    qkv_ref[0] = qkv
    for h in range(heads):
        q, k, v = (head(qkv, i * heads + h, hd) for i in range(3))
        s = mm(k, q, TN) * scale
        top = jnp.max(s, axis=0, keepdims=True)
        e = jnp.exp(s - top)
        inv = 1.0 / jnp.sum(e, axis=0, keepdims=True)
        st_ref[0, h:h + 1] = top
        st_ref[0, heads + h:heads + h + 1] = inv
        mix_ref[0, h * hd:(h + 1) * hd] = mm(v, (e * inv).astype(BF16), NN).astype(BF16)
    out = mm(mix_ref[0], w[3 * hw:4 * hw], TN)

    @pl.when(step == 0)
    def _():
        acc_ref[...] = out

    @pl.when(step > 0)
    def _():
        acc_ref[...] += out

    @pl.when(step == size - 1)
    def _():
        gw1.forward()
        gdo.start()

        def body(c, rows):
            mid = (pair_rows(x_all, c) + acc_ref[rows] + bo_ref[...].astype(F32)).astype(BF16)
            xm_ref[rows] = mid
            xhat, _ = norm_rows(mid.astype(F32))
            h2_ref[rows] = (xhat * g2_ref[...] + c2_ref[...]).astype(BF16)

        pair_chunks(size, tok, body)
        gw1.near()
        gw1.far()
        gdo.forward()
        gdo.near()
        gdo.far()
        for g in (gw1, gdo):
            g.received(*range(6, Gather.COPIES))
        for g in (gw, gw1, gdo):
            g.sent()
        for c in (out_x, out_w, out_w1, out_do):
            c.wait()
        for i in range(1, size):
            out_block(i).wait()


def whole(*shape):
    return pl.BlockSpec(shape, lambda i: (0,) * len(shape), pipeline_mode=pl.Buffered(1))


def block(index, *shape):
    return pl.BlockSpec((1,) + shape, lambda i: (index(i),) + (0,) * len(shape))


def dma(k):
    return pltpu.SemaphoreType.DMA((k,))


def kernel_params(collective_id):
    return pltpu.CompilerParams(dimension_semantics=("arbitrary",), vmem_limit_bytes=67_043_328,
                                collective_id=collective_id, has_side_effects=True)


ANY = pl.BlockSpec(memory_space=pl.ANY)


def front(x, wloc, ln1_gain, ln1_bias, b_o, ln2_gain, ln2_bias, w_1, d_out, heads, hd):
    rows, width = wloc.shape
    imgs, tok, _ = x.shape
    size = imgs
    n = size * tok
    hw = heads * hd
    order = lambda i: arrival(i, size)
    row = whole(1, width)
    bf = lambda *shape: jax.ShapeDtypeStruct(shape, BF16)
    copies = 3 * Gather.COPIES + Exchange.COPIES
    return pl.pallas_call(
        functools.partial(front_kernel, heads, hd, size),
        grid=(size,),
        in_specs=[ANY, whole(rows, width), row, row, row, row, row, whole(*w_1.shape), ANY],
        out_specs=[block(order, 3 * hw, n), block(order, hw, n), block(order, 2 * heads, n),
                   whole(n, width), whole(n, width), whole(n, width), ANY, ANY, ANY, ANY],
        out_shape=[bf(size, 3 * hw, n), bf(size, hw, n), jax.ShapeDtypeStruct((size, 2 * heads, n), F32), bf(n, width), bf(n, width),
                   bf(n, width), bf(size, tok, width), bf(size, rows, width), bf(imgs, n, width), bf(size, *w_1.shape)],
        scratch_shapes=[pltpu.VMEM((size, rows, width), BF16), pltpu.VMEM((size, tok, width), BF16), pltpu.VMEM((2, tok, width), BF16),
                        pltpu.VMEM((n, width), F32), pltpu.VMEM(d_out.shape, BF16), dma(6), dma(size), dma(copies), dma(copies)],
        compiler_params=kernel_params(1),
        name="front",
    )(x, wloc, ln1_gain[None], ln1_bias[None], b_o[None], ln2_gain[None], ln2_bias[None], w_1, d_out)


def gelu_and_slope(u):
    c = math.sqrt(2.0 / math.pi)
    u2 = u * u
    t = jnp.tanh(c * (u + 0.044715 * (u2 * u)))
    half = 0.5 * (1.0 + t)
    slope = half + 0.5 * u * (1.0 - t * t) * (c * (1.0 + (3.0 * 0.044715) * u2))
    return u * half, slope


def block_of_step(j, size):
    me = lax.axis_index('tp')
    chips = size // 2
    off = jnp.where(j < 2, 2, jnp.where(j < 4, 1, jnp.where(j < 6, 3, 0)))
    chip = lax.rem(lax.div(me, 2) + off, chips)
    core = lax.rem(me, 2)
    side = jnp.where(lax.rem(j, 2) == 0, 1 - core, core)
    return 2 * chip + side


def back_kernel(heads, hd, size, h2_ref, xm_ref, dself_ref, w1b_ref, b_ref, w2_ref, g2_ref, b2_ref,
                h_ref, w_ref, qkv_ref, mix_ref, st_ref, do_ref, w1_ref, b1_ref, x3_ref, gain_ref,
                g_ref, gw1_ref, gw2_ref, gb1_ref, gx_ref, vec_ref, yo_ref, h2a_ref, w2a_ref,
                w2_buf, dm_ref, dm3_ref, y3_ref, h_buf, dqkv_ref, dh_ref, gx_own, v_own, v_all, via_y, via_g,
                outs, pair_in, opp_l, opp_r, near_l, near_r, acc, loc_sem, h_sem, send_sem, recv_sem):
    hw = heads * hd
    half = 2 * hw
    scale = 1.0 / math.sqrt(hd)
    step = pl.program_id(0)
    j = step - size
    m = j - size
    me, right, left, _ = ring(size)
    partner = swap_core(me)
    n, width = h_ref.shape
    rows = outs.shape[1]
    tok = x3_ref.shape[1]
    mlp = w2_ref.shape[0]
    sems = send_sem, recv_sem
    own = 2
    gw2 = Gather(size, lambda h: w2_ref.at[cut(mlp)[h]], lambda d, h: w2a_ref.at[d, cut(mlp)[h]], sems, 0)
    gh2 = Gather(size, lambda h: h2_ref.at[cut(n)[h]], lambda d, h: h2a_ref.at[d, cut(n)[h]], sems, Gather.COPIES)
    base = 2 * Gather.COPIES
    ex_y = Exchange(size, lambda d: y3_ref.at[d], lambda d: yo_ref.at[d], via_y, sems, base)
    base += Exchange.COPIES
    ex_g = Exchange(size, lambda d: gx_own.at[d], lambda d: gx_ref.at[d], via_g, sems, base)
    base += Exchange.COPIES
    local = lambda src, dst, i: pltpu.make_async_copy(src, dst, loc_sem.at[i])
    out_h2 = local(h2_ref, h2a_ref.at[me], 0)
    y_local, gx_local = local(y3_ref.at[me], yo_ref.at[me], 1), local(gx_own.at[me], gx_ref.at[me], 2)

    def numbered(src, dst, i, dev):
        return push(src, dst, send_sem.at[base + i], recv_sem.at[base + i], dev)

    def pair_copy(t):
        return numbered(outs.at[t % own], pair_in.at[t % own], t, partner)

    pairs = size // 2
    lo, hi = pl.ds(0, half), pl.ds(half, rows - half)
    one, two = own + 1, own + 2
    opp_right = lambda: numbered(outs.at[own, lo], opp_l, pairs, right)
    opp_left = lambda: numbered(outs.at[own, hi], opp_r, pairs + 1, left)
    right_hi = lambda: numbered(outs.at[one, hi], near_l.at[hi], pairs + 2, right)
    right_lo = lambda: numbered(outs.at[one, lo], near_l.at[lo], pairs + 3, right)
    left_lo = lambda: numbered(outs.at[two, lo], near_r.at[lo], pairs + 4, left)
    left_hi = lambda: numbered(outs.at[two, hi], near_r.at[hi], pairs + 5, left)

    def v_copy(dev, slot):
        return push(v_own, v_all.at[slot], send_sem.at[base + 2 * size + dev], recv_sem.at[base + 2 * size + slot], dev)

    def h_copy(i):
        slot = lax.rem(i, 2)
        return pltpu.make_async_copy(h2a_ref.at[i], h_buf.at[slot], h_sem.at[slot])

    @pl.when(step == 0)
    def _():
        out_h2.start()
        greet_all(size)
        gw2.start()
        w2_buf[...] = w2_ref[...]

    gw2.follow(step, gh2.start)

    @pl.when(step < size)
    def _():
        @pl.when(step > 0)
        def _():
            c = local(w2a_ref.at[arrival(step, size)], w2_buf, 3)
            c.start()
            c.wait()

        w2 = w2_buf[...]
        u = (mm(h2_ref[...], w1b_ref[0], NN) + b_ref[0, 0:1, 3 * hw:3 * hw + mlp].astype(F32)).astype(BF16).astype(F32)
        dg = mm(dself_ref[0], w2, NT).astype(BF16).astype(F32)
        g, slope = gelu_and_slope(u)
        ypart = mm(g.astype(BF16), w2, NN)
        dpart = mm((dg * slope).astype(BF16), w1b_ref[0], NT)

        @pl.when(step == 0)
        def _():
            acc[:n] = ypart
            dh_ref[...] = dpart

        @pl.when(step > 0)
        def _():
            acc[:n] += ypart
            dh_ref[...] += dpart

    @pl.when(j == -1)
    def _():
        v_own[...] = jnp.zeros_like(v_own)

        def body(c, part):
            mid = xm_ref[part].astype(F32)
            y = mid + acc[part] + b2_ref[...].astype(F32)
            xhat, inv = norm_rows(mid)
            dh = dh_ref[part].astype(BF16).astype(F32)
            do = dself_ref[0, part].astype(F32)
            dm = do + norm_rows_pull(xhat, inv, dh, g2_ref[...])
            dm_ref[part] = dm.astype(BF16)
            for side in range(2):
                tokens = slice(side * tok, (side + 1) * tok)
                y3_ref[2 * c + side] = y[tokens].astype(BF16)
                dm3_ref[2 * c + side] = dm[tokens].astype(BF16)
            for i, v in enumerate((dh * xhat, dh, dm.astype(BF16).astype(F32), do)):
                v_own[2 + i:3 + i] += jnp.sum(v, axis=0, keepdims=True)

        pair_chunks(size, tok, body)
        gw2.sent()
        gh2.forward()

    @pl.when((j >= 0) & (j < size))
    def _():
        d_mix = mm(w_ref[0, 3 * hw:4 * hw], dm_ref[...], NT).astype(BF16)
        qkv = qkv_ref[0]
        for h in range(heads):
            q, k, v = (head(qkv, i * heads + h, hd) for i in range(3))
            da = head(d_mix, h, hd)
            s = mm(k, q, TN) * scale
            p = jnp.exp(s - st_ref[0, h:h + 1]) * st_ref[0, heads + h:heads + h + 1]
            dp = mm(v, da, TN).astype(BF16).astype(F32)
            ds = (p * (dp - jnp.sum(p * dp, axis=0, keepdims=True)) * scale).astype(BF16)
            for i, z in enumerate((mm(k, ds, NN), mm(q, ds, NT), mm(da, p.astype(BF16), NT))):
                at = i * hw + h * hd
                dqkv_ref[at:at + hd] = z.astype(BF16)
        dqkv = dqkv_ref[...]
        part = mm(dqkv, w_ref[0, :3 * hw], TN)

        @pl.when(j == 0)
        def _():
            dh_ref[...] = part

        @pl.when(j > 0)
        def _():
            dh_ref[...] += part

        for t in range(own, pairs):
            @pl.when(j == 2 * t)
            def _():
                pair_copy(t - own).wait_send()

        @pl.when(j == size - 1)
        def _():
            opp_right().wait_send()
            opp_left().wait_send()

        turn = lax.div(j, 2)
        out = outs.at[jnp.where(lax.rem(j, 2) == 0, lax.rem(turn, own), own + lax.rem(turn, pairs - 1))]
        out[:3 * hw] = mm(dqkv, h_ref[...], NN)
        out[3 * hw:4 * hw] = mm(mix_ref[0], dm_ref[...], NN)
        sums = mm(jnp.ones((BIAS_ROWS, n), BF16), dqkv, NT)
        out[4 * hw:] = jnp.concatenate([sums, jnp.zeros((BIAS_ROWS, width - 3 * hw), F32)], axis=1)

        for t in range(pairs):
            @pl.when(j == 2 * t)
            def _():
                pair_copy(t).start()

            @pl.when(j == 2 * t + 1)
            def _():
                pair_copy(t).wait_recv()
                outs[own + t % (pairs - 1)] += pair_in[t % own]

        @pl.when(j == 1)
        def _():
            opp_right().start()
            opp_left().start()

        @pl.when(j == 3)
        def _():
            right_hi().start()
            gh2.near()

        @pl.when(j == 5)
        def _():
            left_lo().start()

        @pl.when(j == size - 2)
        def _():
            gh2.far()

        @pl.when(j == size - 1)
        def _():
            opp_right().wait_recv()
            outs[one, lo] += opp_l[...]
            right_lo().start()
            opp_left().wait_recv()
            outs[two, hi] += opp_r[...]
            left_hi().start()
            ex_y.start()
            y_local.start()

    @pl.when(m == 0)
    def _():
        gh2.received(*range(6, Gather.COPIES))
        out_h2.wait()
        h_copy(0).start()

        @pl.loop(0, size)
        def _(dev):
            dh = dh_ref[pl.ds(pl.multiple_of(dev * tok, 8), tok)].astype(BF16).astype(F32)
            xhat, inv = norm_rows(x3_ref[dev].astype(F32))
            gx_own[dev] = (dm3_ref[dev].astype(F32) + norm_rows_pull(xhat, inv, dh, gain_ref[...])).astype(BF16)
            v_own[0:1] += jnp.sum(dh * xhat, axis=0, keepdims=True)
            v_own[1:2] += jnp.sum(dh, axis=0, keepdims=True)

        for r in range(1, size):
            v_copy(lax.rem(me + r, size), me).start()
        ex_g.start()
        gx_local.start()
        v_all[me] = v_own[...]

    @pl.when(m >= 0)
    def _():
        h_copy(m).wait()

        @pl.when(m < size - 1)
        def _():
            h_copy(m + 1).start()

        h2 = h_buf[lax.rem(m, 2)]
        do = do_ref[0]
        u = (mm(w1_ref[...], h2, NT) + b1_ref[...]).astype(BF16).astype(F32)
        dg = mm(w2_ref[...], do, NT).astype(BF16).astype(F32)
        g, slope = gelu_and_slope(u)
        du = (dg * slope).astype(BF16)
        g1 = mm(du, h2, NN)
        g2 = mm(g.astype(BF16), do, NN)
        gb = jnp.sum(du.astype(F32), axis=1, keepdims=True)

        @pl.when(m == 0)
        def _():
            acc[:mlp] = g1
            acc[mlp:] = g2
            gb1_ref[...] = gb

        @pl.when(m > 0)
        def _():
            acc[:mlp] += g1
            acc[mlp:] += g2
            gb1_ref[...] += gb

    @pl.when(m == size - 1)
    def _():
        gw1_ref[...] = acc[:mlp].astype(BF16)
        gw2_ref[...] = acc[mlp:].astype(BF16)
        ring_copies = (right_hi(), right_lo(), left_lo(), left_hi())
        for c in ring_copies:
            c.wait_recv()
        ex_y.forward()
        ex_g.forward()
        g_ref[...] = (outs[own] + near_l[...] + near_r[...]).astype(BF16)
        for c in ring_copies + (pair_copy(pairs - 2), pair_copy(pairs - 1)):
            c.wait_send()
        gh2.sent()
        for r in range(1, size):
            dev = lax.rem(me + r, size)
            v_copy(dev, dev).wait()
        total = v_all[0]
        for i in range(1, size):
            total += v_all[i]
        vec_ref[...] = total
        ex_y.close()
        ex_g.close()
        gx_local.wait()
        y_local.wait()


def back(h_two, x_mid, d_out_all, w1_all, wcat, w_2, gain2, b_2, h_one, qkv, mix, stats, w1t, b1_col, x3, gain1, heads, hd):
    size, rows, width = wcat.shape
    n = h_one.shape[0]
    mlp = w_2.shape[0]
    hw = heads * hd
    first = lambda i: arrival(jnp.minimum(i, size - 1), size)
    second = lambda i: block_of_step(jnp.clip(i - size, 0, size - 1), size)
    third = lambda i: jnp.maximum(i - 2 * size, 0)
    buf = lambda *shape: pltpu.VMEM(shape, F32)
    half_buf = lambda *shape: pltpu.VMEM(shape, BF16)
    bf = lambda *shape: jax.ShapeDtypeStruct(shape, BF16)
    row = whole(1, width)
    copies = 2 * Gather.COPIES + 2 * Exchange.COPIES + 3 * size
    half = 2 * hw
    tokens = x3.shape[1:]
    return pl.pallas_call(
        functools.partial(back_kernel, heads, hd, size),
        grid=(3 * size,),
        in_specs=[whole(n, width), whole(n, width),
                  pl.BlockSpec((1, n, width), lambda i: (lax.axis_index('tp'), 0, 0), pipeline_mode=pl.Buffered(1)),
                  block(first, width, mlp),
                  pl.BlockSpec((1, BIAS_ROWS, width), lambda i: (first(i), rows // BIAS_ROWS - 1, 0)),
                  whole(mlp, width), row, row,
                  whole(n, width), block(second, rows, width), block(second, 3 * hw, n), block(second, hw, n), block(second, 2 * heads, n),
                  block(third, n, width), whole(mlp, width), whole(mlp, 1), whole(*x3.shape), row],
        out_specs=[whole(rows, width), whole(mlp, width), whole(mlp, width), whole(mlp, 1), ANY, whole(8, width), ANY, ANY, ANY],
        out_shape=[bf(rows, width), bf(mlp, width), bf(mlp, width), jax.ShapeDtypeStruct((mlp, 1), F32), bf(*x3.shape),
                   jax.ShapeDtypeStruct((8, width), F32), bf(*x3.shape), bf(size, n, width), bf(size, mlp, width)],
        scratch_shapes=[half_buf(mlp, width), half_buf(n, width), half_buf(*x3.shape), half_buf(*x3.shape), half_buf(2, n, width),
                        half_buf(3 * hw, n), buf(n, width), half_buf(*x3.shape), buf(8, width), buf(size, 8, width),
                        half_buf(2, *tokens), half_buf(2, *tokens), buf(size // 2 + 1, rows, width), buf(2, rows, width),
                        buf(half, width), buf(rows - half, width), buf(rows, width), buf(rows, width), buf(2 * mlp, width),
                        dma(4), dma(2), dma(copies), dma(copies)],
        compiler_params=kernel_params(2),
        name="back",
    )(h_two, x_mid, d_out_all, w1_all, wcat, w_2, gain2[None], b_2[None], h_one, wcat, qkv, mix, stats, d_out_all, w1t, b1_col,
      x3, gain1[None])


def solution(mesh):
    act_spec = P('dp', 'tp', None)
    replicated = P()
    head_w = P(None, 'tp', None)
    head_b = P('tp', None)
    grad_head_w = P('dp', 'tp', None)
    grad_head_b = P(('dp', 'tp'), None)
    grad_vec = P('dp')
    in_specs = (act_spec, act_spec, replicated, replicated, head_w, head_b, head_w, head_w, head_b,
                P('tp', None, None), replicated, replicated, replicated, P(None, 'tp'), P('tp'), P('tp', None), replicated)
    out_specs = (act_spec, act_spec, grad_vec, grad_vec, grad_head_w, grad_head_b, grad_head_w, grad_head_w, grad_head_b,
                 P(('dp', 'tp'), None, None), grad_vec, grad_vec, grad_vec, P('dp', 'tp'), P(('dp', 'tp')),
                 P(('dp', 'tp'), None), grad_vec)

    def layer_step(x, d_out, ln1_gain, ln1_bias, w_q, b_q, w_k, w_v, b_v, w_o, b_o, ln2_gain, ln2_bias, w_1, b_1, w_2, b_2):
        width = x.shape[-1]
        heads_loc, hd = w_q.shape[1:]
        hw = heads_loc * hd
        flat = lambda w: w.reshape(width, hw).T
        bias_row = jnp.concatenate([b_q.reshape(hw), jnp.zeros((hw,), BF16), b_v.reshape(hw), b_1])
        bias_rows = jnp.zeros((BIAS_ROWS, width), BF16).at[0, :bias_row.shape[0]].set(bias_row)
        wloc = jnp.concatenate([flat(w_q), flat(w_k), flat(w_v), w_o.reshape(hw, width), bias_rows])
        qkv, mixed, stats, h_one, x_mid, h_two, x_img, wcat, d_out_all, w1_all = front(
            x, wloc, ln1_gain, ln1_bias, b_o, ln2_gain, ln2_bias, w_1, d_out, heads_loc, hd)
        g_all, gw1, grad_w_2, gb1, grad_x, vec, y_out, _, _ = back(
            h_two, x_mid, d_out_all, w1_all, wcat, w_2, ln2_gain, b_2, h_one, qkv, mixed, stats, w_1.T,
            b_1.astype(F32)[:, None], x_img, ln1_gain, heads_loc, hd)
        grad_w_1 = gw1.T
        grad_b_1 = gb1[:, 0].astype(BF16)
        gb = g_all[4 * hw, :3 * hw]
        grad_b_q = gb[:hw].reshape(b_q.shape)
        grad_b_v = gb[2 * hw:].reshape(b_v.shape)
        gq, gk, gv = (g_all[i * hw:(i + 1) * hw].T.reshape(w_q.shape) for i in range(3))
        grad_w_o = g_all[3 * hw:4 * hw].reshape(w_o.shape)
        return (y_out, grad_x, vec[0], vec[1], gq, grad_b_q, gk, gv, grad_b_v, grad_w_o,
                vec[4].astype(BF16), vec[2], vec[3], grad_w_1, grad_b_1, grad_w_2, vec[5].astype(BF16))

    return jax.shard_map(layer_step, mesh=mesh, in_specs=in_specs, out_specs=out_specs, check_vma=False)
```

time: 858 us -> 349 us (0.41)
  waiting for transfers between devices: 546 us -> 0 us
  Pallas kernels: 0 us -> 323 us
  matrix products: 225 us -> 0 us
  other arithmetic: 34.8 us -> 3.04 us
  blocking collectives: 21.3 us -> 0 us
  between operations: 14.9 us -> 0.7 us
  local copies, waits for them, and re-layouts: 8.94 us -> 21.8 us
    reduce_scatter x4 -> x0, waiting for transfers between devices: 345 us -> none  [scatter_sum(): return lax.psum_scatter(part_sum, 'tp', scatter_dimension=1, tiled=True)]
    pallas_call x0 -> x2, Pallas kernels: none -> 323 us  [the longest x1 180 us: back(): pl.pallas_call(functools.partial(back_kernel, heads, hd, size), grid=(3 *...]
    dot_general x23 -> x0, matrix products: 211 us -> none  [the longest x2 30.6 us: attention_core(): jnp.einsum('bqhd,bkhd->bhqk', queries, keys, preferred_element_type=jnp.f...]
    all_gather x4 -> x0, waiting for transfers between devices: 200 us -> none  [gather_tokens(): return lax.all_gather(local_rows, 'tp', axis=1, tiled=True)]
    psum x1 -> x0, blocking collectives: 21.3 us -> none  [layer_step(): lax.psum(jnp.stack([g_ln1_gain, g_ln1_bias, token_sum(d_mid), g_ln2_gain,...]
    reduce_sum x9 -> x0, other arithmetic: 19.2 us -> none  [the longest x4 8.64 us: layer_norm(): return centered * lax.rsqrt(variance + LN_EPS) * ln_gain + ln_bias]
    convert_element_type x9 -> x1, other arithmetic: 15.5 us -> 1.66 us  [layer_step(): grad_b_1 = gb1[:, 0].astype(BF16)]
    sub x1 -> x0, matrix products: 13.5 us -> none  [attention_core(): probs = jax.nn.softmax(scores, axis=-1).astype(jnp.bfloat16)]
  transfers between devices with their start and end apart: 8 -> 0, of which waited for: 8 -> 0; matrix products, arithmetic and copies ran while one was open for 7% -> 0% of each run, Pallas kernels for 0% -> 0%
where the time goes in v2:
time: 349 us
  Pallas kernels  323 us (93%)
  local copies, waits for them, and re-layouts  21.8 us (6%)
    pallas_call x1, Pallas kernels, back(): pl.pallas_call(functools.partial(back_kernel, heads, hd, size), grid=(3 *...  180 us
    pallas_call x1, Pallas kernels, front(): pl.pallas_call(functools.partial(front_kernel, heads, hd, size), grid=(si...  143 us
    unnamed x27, local copies, waits for them, and re-layouts  10.9 us

profile of v2, /device:TPU:81, one launch (start us, length us, event | category | flops | bytes accessed | tf_op | source)
XLA Modules:
  0.0 348.6 jit_solution(9801566200311289001)
XLA Ops:
  0.7 0.7 reshape.111
  1.4 0.7 reshape.112
  2.1 0.7 pad_maximum_fusion
  2.8 0.7 broadcast_in_dim.38
  3.5 1.3 broadcast_in_dim.32.bo_ref
  4.8 1.3 broadcast_in_dim.35.b2_ref
  6.1 0.9 copy.37.b1_ref
  6.9 0.0 copy-start.4
  6.9 0.0 copy-start.5
  6.9 0.0 copy-start.6
  6.9 2.3 copy.36
  9.3 0.0 copy-start.7
  9.3 0.0 copy-done.4
  9.3 0.7 constant_dynamic-update-slice_fusion.3
  10.0 0.0 copy-done.5
  10.0 0.7 constant_dynamic-update-slice_fusion.2
  10.7 0.0 copy-done.6
  10.7 0.7 constant_dynamic-update-slice_fusion.1
  11.4 0.0 copy-done.7
  11.4 0.7 constant_dynamic-update-slice_fusion
  12.2 0.6 pad_dynamic-update-slice_fusion.wl_ref
  12.8 142.7 %front.1 = (bf16[8,384,576]{2,1,0:T(8,128)(2,1)}, bf16[8,128,576]{2,1,0:T(8,128)(2,1)}, f32[8,4,576]{2,1,0:T(4,128)}, bf16[576,1024]{1,0:T(8,128)(2,1)}, bf16[57...) custom-call(bf16[8,72,1024]{2,1,0:T(8,128)(2,1)} %x_ref.1, ...), custom_call_target="tpu_custom_call" | custom-call | tf_op jit(solution)/shard_map/front/pallas_call | solution.py:301
  155.5 180.5 %back.1 = (bf16[528,1024]{1,0:T(8,128)(2,1)}, bf16[512,1024]{1,0:T(8,128)(2,1)}, bf16[512,1024]{1,0:T(8,128)(2,1)}, f32[512,1]{1,0:T(8,128)}, bf16[8,72,1024]{2,...) custom-call(bf16[576,1024]{1,0:T(8,128)(2,1)} %get-tuple-element.46., ...), custom_call_target="tpu_custom_call" | custom-call | tf_op jit(solution)/shard_map/back/pallas_call | solution.py:617
  336.0 1.7 convert_reduce_fusion
  337.6 0.0 copy-start.8
  337.6 0.7 slice_reduce_fusion.2
  338.3 0.0 copy-start.3
  338.3 2.3 fusion
  340.6 0.6 reshape.118
  341.2 0.6 reshape.115
  341.8 0.0 copy-done.8
  341.8 0.0 copy-start.1
  341.8 0.6 fusion.1
  342.4 0.6 slice_reduce_fusion
  343.0 0.0 copy-done.3
  343.0 1.3 copy.38
  344.3 0.0 copy-done.1
  344.3 0.0 copy-start
  344.3 1.0 copy.46
  345.3 0.7 copy-done
  346.0 0.0 copy-start.2
  346.0 1.0 copy.47
  347.0 0.6 copy-done.2
  347.7 1.0 copy.48
  (3 shorter events, 0.0 us)
Async XLA Ops:
  6.9 2.3 copy-start.4
  6.9 3.1 copy-start.5
  6.9 3.8 %copy-start.6 = (bf16[1024,2,64]{0,2,1:T(8,128)(2,1)S(1)}, bf16[1024,2,64]{0,2,1:T(8,128)(2,1)}, u32[]{:S(2)}) copy-start(bf16[1024,2,64]{0,2,1:T(8,128)(2,1)} %param.26) | copy-start | bytes 786436
  9.3 2.2 copy-start.7
  337.6 4.2 %copy-start.8 = (f32[8,1024]{1,0:T(8,128)S(1)}, f32[8,1024]{1,0:T(8,128)}, u32[]{:S(2)}) copy-start(f32[8,1024]{1,0:T(8,128)} %get-tuple-element.58) | copy-start | bytes 98308
  338.3 4.7 %copy-start.3 = (bf16[512,1024]{1,0:T(8,128)(2,1)S(1)}, bf16[512,1024]{1,0:T(8,128)(2,1)}, u32[]{:S(2)}) copy-start(bf16[512,1024]{1,0:T(8,128)(2,1)} %get-tuple-element.60) | copy-start | bytes 3145732
  341.8 2.6 copy-start.1
  344.3 1.7 copy-start
  346.0 1.7 copy-start.2

commit v3 on v2

v3 whole, which is shorter than its diff:
```python
import functools
import math
import jax
import jax.numpy as jnp
from jax import lax
from jax.experimental import pallas as pl
from jax.experimental.pallas import tpu as pltpu
from jax.sharding import PartitionSpec as P

LN_EPS = 1e-6
F32 = jnp.float32
BF16 = jnp.bfloat16
NN = (((1,), (0,)), ((), ()))
NT = (((1,), (1,)), ((), ()))
TN = (((0,), (0,)), ((), ()))
BIAS_ROWS = 16


def mm(a, b, dims):
    return lax.dot_general(a, b, dims, preferred_element_type=F32)


def push(src, dst, ssem, rsem, dev):
    return pltpu.make_async_remote_copy(src_ref=src, dst_ref=dst, send_sem=ssem, recv_sem=rsem,
                                        device_id={'tp': dev}, device_id_type=pl.DeviceIdType.MESH)


def greet_all(size):
    me = lax.axis_index('tp')
    barrier = pltpu.get_barrier_semaphore()
    for r in range(1, size):
        pl.semaphore_signal(barrier, inc=1, device_id={'tp': lax.rem(me + r, size)}, device_id_type=pl.DeviceIdType.MESH)
    pl.semaphore_wait(barrier, size - 1)


def swap_core(dev):
    return dev + 1 - 2 * lax.rem(dev, 2)


def ring(size):
    me = lax.axis_index('tp')
    return me, lax.rem(me + 2, size), lax.rem(me + size - 2, size), lax.rem(me + size // 2, size)


class Gather:
    COPIES = 14

    def __init__(self, size, src, dst, sems, off):
        me, right, left, opp = ring(size)
        partner = swap_core(me)
        plan = [(me, 0, right), (me, 1, right), (left, 0, right), (me, 1, left), (me, 0, left), (right, 1, left)]
        plan += [(owner, half, partner) for owner in (me, left, right, opp) for half in range(2)]

        def make(i):
            owner, half, dev = plan[i]
            out = dst(owner, half)
            return push(src(half) if owner is me else out, out, sems[0].at[off + i], sems[1].at[off + i], dev)

        self.copy = make

    def start(self):
        for i in (0, 3, 1, 4, 6, 7):
            self.copy(i).start()

    def forward(self):
        for got, sends in ((0, (2, 8)), (3, (5, 11))):
            self.copy(got).wait_recv()
            for i in sends:
                self.copy(i).start()

    def relay(self, *pairs):
        for got, i in pairs:
            self.copy(got).wait_recv()
            self.copy(i).start()

    def near(self):
        self.relay((1, 9), (4, 10))

    def far(self):
        self.relay((2, 12), (5, 13))

    def received(self, *which):
        for i in which:
            self.copy(i).wait_recv()

    def sent(self):
        for i in range(self.COPIES):
            self.copy(i).wait_send()

    def follow(self, step, *ahead):
        def at(k, *calls):
            @pl.when(step == k)
            def _():
                for call in calls:
                    call()

        at(1, lambda: self.received(6, 7))
        at(2, *ahead, lambda: self.relay((1, 9)))
        at(3, lambda: self.relay((4, 10)))
        at(4, lambda: self.received(8, 9))
        at(5, lambda: self.received(10, 11))
        at(6, self.far)
        at(7, lambda: self.received(12, 13))


class Exchange:
    COPIES = 9

    def __init__(self, size, src, dst, via, sems, off):
        me, right, left, opp = ring(size)
        plan = [(src(opp), via.at[0], left), (src(swap_core(opp)), via.at[1], right)]
        plan += [(src(dev), dst(me), dev) for side in (right, left) for dev in (side, swap_core(side))]
        plan += [(src(swap_core(me)), dst(me), swap_core(me)), (via.at[0], dst(right), left), (via.at[1], dst(left), swap_core(right))]
        self.copy = lambda i: push(*plan[i][:2], sems[0].at[off + i], sems[1].at[off + i], plan[i][2])

    def start(self):
        for i in range(7):
            self.copy(i).start()

    def forward(self):
        for got, i in ((0, 7), (1, 8)):
            self.copy(got).wait_recv()
            self.copy(i).start()

    def close(self):
        for i in range(2, self.COPIES):
            self.copy(i).wait_recv()
        for i in range(self.COPIES):
            self.copy(i).wait_send()


def pair_rows(ref, c):
    return jnp.concatenate([ref[2 * c].astype(F32), ref[2 * c + 1].astype(F32)])


def pair_chunks(size, tok, body):
    pl.loop(0, size // 2)(lambda c: body(c, pl.ds(pl.multiple_of(c * 2 * tok, 16), 2 * tok)))


def cut(rows):
    half = rows // 2 // 16 * 16
    return pl.ds(0, half), pl.ds(half, rows - half)


def head(z, i, hd):
    return z[i * hd:(i + 1) * hd]


def norm_rows(z):
    centered = z - jnp.mean(z, axis=-1, keepdims=True)
    inv = lax.rsqrt(jnp.mean(centered * centered, axis=-1, keepdims=True) + LN_EPS)
    return centered * inv, inv


def norm_rows_pull(xhat, inv, dh, gain):
    dxh = dh * gain
    return inv * (dxh - jnp.mean(dxh, axis=-1, keepdims=True) - xhat * jnp.mean(dxh * xhat, axis=-1, keepdims=True))


def arrival(i, size):
    me = lax.axis_index('tp')
    partner = me + 1 - 2 * lax.rem(me, 2)
    hop = jnp.where(i < 2, 0, jnp.where(i >= 6, size // 2, jnp.where(lax.rem(i, 2) == 0, size - 2, 2)))
    base = jnp.where((i == 1) | (i == 4) | (i == 5) | (i == 7), partner, me)
    return lax.rem(base + hop, size)


def gelu_and_slope(u):
    c = math.sqrt(2.0 / math.pi)
    u2 = u * u
    t = jnp.tanh(c * (u + 0.044715 * (u2 * u)))
    half = 0.5 * (1.0 + t)
    slope = half + 0.5 * u * (1.0 - t * t) * (c * (1.0 + (3.0 * 0.044715) * u2))
    return u * half, slope


def front_kernel(heads, hd, size, x_ref, wq_ref, wk_ref, wv_ref, wo_ref, bq_ref, bv_ref, b1_ref,
                 g1_ref, c1_ref, g2_ref, c2_ref, bo_ref, b2_ref, w1_ref, w2_ref, do_ref,
                 qkv_ref, mix_ref, st_ref, h1_ref, y_ref, dm_ref, sums_ref, w1t_ref, xi_ref, wa_ref, doa_ref, h2a_ref,
                 wl_ref, w_all, w1_all, w2_all, x_all, via, acc_ref, dacc, own_do, d_img, xm_ref, h2_ref, loc_sem, out_sem, send_sem, recv_sem):
    hw = heads * hd
    scale = 1.0 / math.sqrt(hd)
    step = pl.program_id(0)
    k = step - size
    mlp = w2_ref.shape[0]
    me = lax.axis_index('tp')
    imgs, tok, width = x_ref.shape
    n = h1_ref.shape[0]
    g1, c1, g2, c2 = g1_ref[...], c1_ref[...], g2_ref[...], c2_ref[...]
    bo, b2 = (r[...].astype(F32).reshape(1, width) for r in (bo_ref, b2_ref))
    rows = wl_ref.shape[0]
    sems = send_sem, recv_sem
    images = pl.ds(0, imgs // 2), pl.ds(imgs // 2, imgs // 2)
    mine = lambda dev: pl.ds(pl.multiple_of(dev * tok, 8), tok)
    gw = Gather(size, lambda h: wl_ref.at[cut(rows)[h]], lambda d, h: w_all.at[d, cut(rows)[h]], sems, 0)
    gw1 = Gather(size, lambda h: w1_ref.at[cut(width)[h]], lambda d, h: w1_all.at[d, cut(width)[h]], sems, Gather.COPIES)
    gdo = Gather(size, lambda h: do_ref.at[images[h]], lambda d, h: doa_ref.at[images[h], mine(d)], sems, 2 * Gather.COPIES)
    gw2 = Gather(size, lambda h: w2_ref.at[cut(mlp)[h]], lambda d, h: w2_all.at[d, cut(mlp)[h]], sems, 3 * Gather.COPIES)
    gh2 = Gather(size, lambda h: h2_ref.at[cut(n)[h]], lambda d, h: h2a_ref.at[d, cut(n)[h]], sems, 4 * Gather.COPIES)
    ex = Exchange(size, lambda d: x_ref.at[d], lambda d: x_all.at[d], via, sems, 5 * Gather.COPIES)
    local = lambda src, dst, i: pltpu.make_async_copy(src, dst, loc_sem.at[i])
    in_x, in_do = local(x_ref.at[me], x_all.at[me], 0), local(do_ref, own_do, 1)
    out_w, out_h2 = local(wl_ref, wa_ref.at[me], 2), local(h2_ref, h2a_ref.at[me], 3)
    in_img = local(doa_ref.at[me], d_img, 6)
    out_x, out_do = local(x_all, xi_ref, 4), local(own_do, doa_ref.at[:, mine(me)], 5)

    def out_block(i):
        dev = arrival(i, size)
        return pltpu.make_async_copy(w_all.at[dev], wa_ref.at[dev], out_sem.at[i])

    @pl.when(step == 0)
    def _():
        in_x.start()
        in_do.start()
        greet_all(size)
        ex.start()
        for i, part in enumerate((wq_ref, wk_ref, wv_ref, wo_ref)):
            wl_ref[i * hw:(i + 1) * hw] = part[...]
        zeros = jnp.zeros((1, hw), F32)
        pieces = [r[h:h + 1].astype(F32) for r in (bq_ref, bv_ref) for h in range(heads)]
        line = jnp.concatenate(pieces[:heads] + [zeros] + pieces[heads:] + [b1_ref[...].astype(F32).reshape(1, mlp)]
                               + [zeros] * ((width - 3 * hw - mlp) // hw), axis=1)
        wl_ref[4 * hw:] = jnp.where(lax.broadcasted_iota(jnp.int32, (BIAS_ROWS, width), 0) == 0, line, 0.0).astype(BF16)
        ex.forward()
        gw.start()
        out_w.start()
        w_all[me] = wl_ref[...]
        in_x.wait()
        ex.close()
        out_x.start()

        def body(c, rows):
            xhat, _ = norm_rows(pair_rows(x_all, c))
            h1_ref[rows] = (xhat * g1 + c1).astype(BF16)

        pair_chunks(size, tok, body)
        in_do.wait()
        out_do.start()

    gw.follow(step, gw.forward, gdo.start)

    @pl.when((step > 0) & (k < 0))
    def _():
        out_block(step).start()

    @pl.when(k < 0)
    def _():
        w = w_all.at[arrival(step, size)]
        bias = mm(w[4 * hw:, :3 * hw], jnp.ones((BIAS_ROWS, n), BF16), TN)
        qkv = (mm(w[:3 * hw], h1_ref[...], NT) + bias).astype(BF16)
        qkv_ref[0] = qkv
        for h in range(heads):
            q, key, v = (head(qkv, i * heads + h, hd) for i in range(3))
            s = mm(key, q, TN) * scale
            top = jnp.max(s, axis=0, keepdims=True)
            e = jnp.exp(s - top)
            inv = 1.0 / jnp.sum(e, axis=0, keepdims=True)
            st_ref[0, h:h + 1] = top
            st_ref[0, heads + h:heads + h + 1] = inv
            mix_ref[0, h * hd:(h + 1) * hd] = mm(v, (e * inv).astype(BF16), NN).astype(BF16)
        out = mm(mix_ref[0], w[3 * hw:4 * hw], TN)

        @pl.when(step == 0)
        def _():
            acc_ref[...] = out

        @pl.when(step > 0)
        def _():
            acc_ref[...] += out

    @pl.when(k == -1)
    def _():
        gdo.forward()
        gw1.start()

        def body(c, rows):
            mid = (pair_rows(x_all, c) + acc_ref[rows] + bo).astype(BF16)
            xm_ref[rows] = mid
            xhat, _ = norm_rows(mid.astype(F32))
            h2_ref[rows] = (xhat * g2 + c2).astype(BF16)

        pair_chunks(size, tok, body)

    @pl.when(k == 0)
    def _():
        out_h2.start()
        w1_all[me] = w1_ref[...]
        w2_all[me] = w2_ref[...]
        w1t_ref[...] = w1_ref[...].T
        gdo.near()
        gdo.far()
        gw1.forward()
        gw2.start()
        gdo.received(*range(6, Gather.COPIES))
        out_do.wait()
        in_img.start()
        in_img.wait()

    gw1.follow(k)
    gw2.follow(k, gw2.forward, gh2.start)

    @pl.when(k >= 0)
    def _():
        dev = arrival(k, size)
        w1, w2 = w1_all[dev], w2_all[dev]
        b1 = w_all[dev, 4 * hw:4 * hw + 1, 3 * hw:3 * hw + mlp].astype(F32)
        u = (mm(h2_ref[...], w1, NN) + b1).astype(BF16).astype(F32)
        dg = mm(d_img[...], w2, NT).astype(BF16).astype(F32)
        g, slope = gelu_and_slope(u)
        ypart = mm(g.astype(BF16), w2, NN)
        dpart = mm((dg * slope).astype(BF16), w1, NT)

        @pl.when(k == 0)
        def _():
            acc_ref[...] = ypart
            dacc[...] = dpart

        @pl.when(k > 0)
        def _():
            acc_ref[...] += ypart
            dacc[...] += dpart

    @pl.when(k == size - 1)
    def _():
        sums_ref[...] = jnp.zeros_like(sums_ref)

        def body(c, part):
            mid = xm_ref[part].astype(F32)
            y_ref[part] = (mid + acc_ref[part] + b2).astype(BF16)
            xhat, inv = norm_rows(mid)
            dh = dacc[part].astype(BF16).astype(F32)
            do = d_img[part].astype(F32)
            dm = (do + norm_rows_pull(xhat, inv, dh, g2)).astype(BF16)
            dm_ref[part] = dm
            for i, v in enumerate((dh * xhat, dh, dm.astype(F32), do)):
                sums_ref[2 + i:3 + i] += jnp.sum(v, axis=0, keepdims=True)

        pair_chunks(size, tok, body)
        gh2.forward()
        gh2.near()
        gh2.far()
        gh2.received(*range(6, Gather.COPIES))
        for g in (gw, gw1, gdo, gw2, gh2):
            g.sent()
        for c in (out_x, out_w, out_h2):
            c.wait()
        for i in range(1, size):
            out_block(i).wait()


def whole(*shape):
    return pl.BlockSpec(shape, lambda i: (0,) * len(shape), pipeline_mode=pl.Buffered(1))


def block(index, *shape):
    return pl.BlockSpec((1,) + shape, lambda i: (index(i),) + (0,) * len(shape))


def dma(k):
    return pltpu.SemaphoreType.DMA((k,))


def kernel_params(collective_id):
    return pltpu.CompilerParams(dimension_semantics=("arbitrary",), vmem_limit_bytes=67_043_328,
                                collective_id=collective_id, has_side_effects=True)


ANY = pl.BlockSpec(memory_space=pl.ANY)


def front(x, weights, biases, gains, sums_bias, w_1, w_2, d_out, heads, hd):
    imgs, tok, width = x.shape
    size = imgs
    n = size * tok
    hw = heads * hd
    mlp = w_2.shape[0]
    rows = 4 * hw + BIAS_ROWS
    order = lambda i: arrival(jnp.minimum(i, size - 1), size)
    bf = lambda *shape: jax.ShapeDtypeStruct(shape, BF16)
    buf = lambda *shape: pltpu.VMEM(shape, BF16)
    copies = 5 * Gather.COPIES + Exchange.COPIES
    return pl.pallas_call(
        functools.partial(front_kernel, heads, hd, size),
        grid=(2 * size,),
        in_specs=[ANY] + [whole(*z.shape) for z in weights + biases + gains + sums_bias] + [ whole(width, mlp), whole(mlp, width), ANY],
        out_specs=[block(order, 3 * hw, n), block(order, hw, n), block(order, 2 * heads, n), whole(n, width), whole(n, width),
                   whole(n, width), whole(8, width), whole(mlp, width), ANY, ANY, ANY, ANY],
        out_shape=[bf(size, 3 * hw, n), bf(size, hw, n), jax.ShapeDtypeStruct((size, 2 * heads, n), F32), bf(n, width), bf(n, width),
                   bf(n, width), jax.ShapeDtypeStruct((8, width), F32), bf(mlp, width),
                   bf(size, tok, width), bf(size, rows, width), bf(imgs, n, width), bf(size, n, width)],
        scratch_shapes=[buf(rows, width), buf(size, rows, width), buf(size, width, mlp), buf(size, mlp, width), buf(size, tok, width), buf(2, tok, width),
                        pltpu.VMEM((n, width), F32), pltpu.VMEM((n, width), F32), buf(*d_out.shape), buf(n, width), buf(n, width),
                        buf(n, width), dma(7), dma(size), dma(copies), dma(copies)],
        compiler_params=kernel_params(1),
        name="front",
    )(x, *weights, *biases, *gains, *sums_bias, w_1, w_2, d_out)


def block_of_step(j, size):
    me = lax.axis_index('tp')
    chips = size // 2
    off = jnp.where(j < 2, 2, jnp.where(j < 4, 1, jnp.where(j < 6, 3, 0)))
    chip = lax.rem(lax.div(me, 2) + off, chips)
    core = lax.rem(me, 2)
    side = jnp.where(lax.rem(j, 2) == 0, 1 - core, core)
    return 2 * chip + side


def back_kernel(heads, hd, size, h_ref, dm_ref, w_ref, qkv_ref, mix_ref, st_ref, h2_ref, do_ref, w1_ref, w2_ref, b_ref,
                x3_ref, dm3_ref, y3_ref, gain_ref, vin_ref,
                g_ref, gw1_ref, gw2_ref, gb1_ref, gx_ref, vec_ref, yo_ref,
                dqkv_ref, dh_ref, gx_own, v_own, v_all, via_y, via_g,
                outs, pair_in, opp_l, opp_r, near_l, near_r, acc, loc_sem, send_sem, recv_sem):
    hw = heads * hd
    half = 2 * hw
    scale = 1.0 / math.sqrt(hd)
    j = pl.program_id(0)
    m = j - size
    me, right, left, _ = ring(size)
    partner = swap_core(me)
    n, width = h_ref.shape
    rows = outs.shape[1]
    tok = x3_ref.shape[1]
    mlp = w2_ref.shape[0]
    sems = send_sem, recv_sem
    own = 2
    base = 0
    ex_y = Exchange(size, lambda d: y3_ref.at[d], lambda d: yo_ref.at[d], via_y, sems, base)
    base += Exchange.COPIES
    ex_g = Exchange(size, lambda d: gx_own.at[d], lambda d: gx_ref.at[d], via_g, sems, base)
    base += Exchange.COPIES
    local = lambda src, dst, i: pltpu.make_async_copy(src, dst, loc_sem.at[i])
    y_local, gx_local = local(y3_ref.at[me], yo_ref.at[me], 1), local(gx_own.at[me], gx_ref.at[me], 2)

    def numbered(src, dst, i, dev):
        return push(src, dst, send_sem.at[base + i], recv_sem.at[base + i], dev)

    def pair_copy(t):
        return numbered(outs.at[t % own], pair_in.at[t % own], t, partner)

    pairs = size // 2
    lo, hi = pl.ds(0, half), pl.ds(half, rows - half)
    one, two = own + 1, own + 2
    opp_right = lambda: numbered(outs.at[own, lo], opp_l, pairs, right)
    opp_left = lambda: numbered(outs.at[own, hi], opp_r, pairs + 1, left)
    right_hi = lambda: numbered(outs.at[one, hi], near_l.at[hi], pairs + 2, right)
    right_lo = lambda: numbered(outs.at[one, lo], near_l.at[lo], pairs + 3, right)
    left_lo = lambda: numbered(outs.at[two, lo], near_r.at[lo], pairs + 4, left)
    left_hi = lambda: numbered(outs.at[two, hi], near_r.at[hi], pairs + 5, left)

    def v_copy(dev, slot):
        return push(v_own, v_all.at[slot], send_sem.at[base + 2 * size + dev], recv_sem.at[base + 2 * size + slot], dev)

    @pl.when(j == 0)
    def _():
        greet_all(size)
        ex_y.start()
        y_local.start()

    @pl.when(j == 1)
    def _():
        ex_y.forward()

    @pl.when(j < size)
    def _():
        d_mix = mm(dm_ref[...], w_ref[0, 3 * hw:4 * hw], NT).astype(BF16).T
        qkv = qkv_ref[0]
        for h in range(heads):
            q, k, v = (head(qkv, i * heads + h, hd) for i in range(3))
            da = head(d_mix, h, hd)
            s = mm(k, q, TN) * scale
            p = jnp.exp(s - st_ref[0, h:h + 1]) * st_ref[0, heads + h:heads + h + 1]
            dp = mm(v, da, TN).astype(BF16).astype(F32)
            ds = (p * (dp - jnp.sum(p * dp, axis=0, keepdims=True)) * scale).astype(BF16)
            dk = mm(ds, q, NT).astype(BF16).T
            dv = mm(p.astype(BF16), da, NT).astype(BF16).T
            for i, z in enumerate((mm(k, ds, NN).astype(BF16), dk, dv)):
                at = i * hw + h * hd
                dqkv_ref[at:at + hd] = z
        dqkv = dqkv_ref[...]
        part = mm(dqkv, w_ref[0, :3 * hw], TN)

        @pl.when(j == 0)
        def _():
            dh_ref[...] = part

        @pl.when(j > 0)
        def _():
            dh_ref[...] += part

        for t in range(own, pairs):
            @pl.when(j == 2 * t)
            def _():
                pair_copy(t - own).wait_send()

        @pl.when(j == size - 1)
        def _():
            opp_right().wait_send()
            opp_left().wait_send()

        turn = lax.div(j, 2)
        out = outs.at[jnp.where(lax.rem(j, 2) == 0, lax.rem(turn, own), own + lax.rem(turn, pairs - 1))]
        out[:3 * hw] = mm(dqkv, h_ref[...], NN)
        out[3 * hw:4 * hw] = mm(mix_ref[0], dm_ref[...], NN)
        sums = mm(jnp.ones((BIAS_ROWS, n), BF16), dqkv, NT)
        out[4 * hw:] = jnp.concatenate([sums, jnp.zeros((BIAS_ROWS, width - 3 * hw), F32)], axis=1)

        for t in range(pairs):
            @pl.when(j == 2 * t)
            def _():
                pair_copy(t).start()

            @pl.when(j == 2 * t + 1)
            def _():
                pair_copy(t).wait_recv()
                outs[own + t % (pairs - 1)] += pair_in[t % own]

        @pl.when(j == 1)
        def _():
            opp_right().start()
            opp_left().start()

        @pl.when(j == 3)
        def _():
            right_hi().start()

        @pl.when(j == 5)
        def _():
            left_lo().start()

        @pl.when(j == size - 1)
        def _():
            opp_right().wait_recv()
            outs[one, lo] += opp_l[...]
            right_lo().start()
            opp_left().wait_recv()
            outs[two, hi] += opp_r[...]
            left_hi().start()

    @pl.when(m == 0)
    def _():
        v_own[...] = vin_ref[...]

        @pl.loop(0, size)
        def _(dev):
            dh = dh_ref[pl.ds(pl.multiple_of(dev * tok, 8), tok)].astype(BF16).astype(F32)
            xhat, inv = norm_rows(x3_ref[dev].astype(F32))
            gx_own[dev] = (dm3_ref[dev].astype(F32) + norm_rows_pull(xhat, inv, dh, gain_ref[...])).astype(BF16)
            v_own[0:1] += jnp.sum(dh * xhat, axis=0, keepdims=True)
            v_own[1:2] += jnp.sum(dh, axis=0, keepdims=True)

        for r in range(1, size):
            v_copy(lax.rem(me + r, size), me).start()
        ex_g.start()
        gx_local.start()
        v_all[me] = v_own[...]

    @pl.when(m == size - 1)
    def _():
        ex_g.forward()

    @pl.when(m >= 0)
    def _():
        h2 = h2_ref[0]
        do = do_ref[0]
        one_row = (lax.broadcasted_iota(jnp.int32, (BIAS_ROWS, n), 0) == 0).astype(F32).astype(BF16)
        b1 = mm(b_ref[0, :, 3 * hw:3 * hw + mlp], one_row, TN)
        u = (mm(w1_ref[...], h2, NT) + b1).astype(BF16).astype(F32)
        dg = mm(w2_ref[...], do, NT).astype(BF16).astype(F32)
        g, slope = gelu_and_slope(u)
        du = (dg * slope).astype(BF16)
        g1 = mm(du, h2, NN)
        g2 = mm(g.astype(BF16), do, NN)
        gb = mm(jnp.ones((8, n), BF16), du, NT)

        @pl.when(m == 0)
        def _():
            acc[:mlp] = g1
            acc[mlp:] = g2
            gb1_ref[...] = gb

        @pl.when(m > 0)
        def _():
            acc[:mlp] += g1
            acc[mlp:] += g2
            gb1_ref[...] += gb

    @pl.when(m == size - 1)
    def _():
        gw1_ref[...] = acc[:mlp].astype(BF16)
        gw2_ref[...] = acc[mlp:].astype(BF16)
        ring_copies = (right_hi(), right_lo(), left_lo(), left_hi())
        for c in ring_copies:
            c.wait_recv()
        g_ref[...] = (outs[own] + near_l[...] + near_r[...]).astype(BF16)
        for c in ring_copies + (pair_copy(pairs - 2), pair_copy(pairs - 1)):
            c.wait_send()
        for r in range(1, size):
            dev = lax.rem(me + r, size)
            v_copy(dev, dev).wait()
        total = v_all[0]
        for i in range(1, size):
            total += v_all[i]
        vec_ref[...] = total
        ex_y.close()
        ex_g.close()
        gx_local.wait()
        y_local.wait()


def back(h_one, d_mid, wcat, qkv, mix, stats, h2_all, d_out_all, w1t, w_2, x3, y_img, gain, sums, heads, hd):
    size, rows, width = wcat.shape
    n = h_one.shape[0]
    mlp = w_2.shape[0]
    hw = heads * hd
    first = lambda i: block_of_step(jnp.minimum(i, size - 1), size)
    second = lambda i: jnp.maximum(i - size, 0)
    buf = lambda *shape: pltpu.VMEM(shape, F32)
    half_buf = lambda *shape: pltpu.VMEM(shape, BF16)
    bf = lambda *shape: jax.ShapeDtypeStruct(shape, BF16)
    copies = 2 * Exchange.COPIES + 3 * size
    half = 2 * hw
    tokens = x3.shape[1:]
    act3 = whole(*x3.shape)
    return pl.pallas_call(
        functools.partial(back_kernel, heads, hd, size),
        grid=(2 * size,),
        in_specs=[whole(n, width), whole(n, width), block(first, rows, width), block(first, 3 * hw, n), block(first, hw, n),
                  block(first, 2 * heads, n), block(second, n, width), block(second, n, width), whole(mlp, width), whole(mlp, width),
                  pl.BlockSpec((1, BIAS_ROWS, width), lambda i: (lax.axis_index('tp'), rows // BIAS_ROWS - 1, 0)),
                  act3, act3, act3, whole(1, width), whole(*sums.shape)],
        out_specs=[whole(rows, width), whole(mlp, width), whole(mlp, width), whole(8, mlp), ANY, whole(*sums.shape), ANY],
        out_shape=[bf(rows, width), bf(mlp, width), bf(mlp, width), jax.ShapeDtypeStruct((8, mlp), F32), bf(*x3.shape),
                   jax.ShapeDtypeStruct(sums.shape, F32), bf(*x3.shape)],
        scratch_shapes=[half_buf(3 * hw, n), buf(n, width), half_buf(*x3.shape), buf(*sums.shape), buf(size, *sums.shape),
                        half_buf(2, *tokens), half_buf(2, *tokens), buf(size // 2 + 1, rows, width), buf(2, rows, width),
                        buf(half, width), buf(rows - half, width), buf(rows, width), buf(rows, width), buf(2 * mlp, width),
                        dma(3), dma(copies), dma(copies)],
        compiler_params=kernel_params(2),
        name="back",
    )(h_one, d_mid, wcat, qkv, mix, stats, h2_all, d_out_all, w1t, w_2, wcat, x3, d_mid.reshape(x3.shape), y_img.reshape(x3.shape),
      gain, sums)


def finish_kernel(heads, hd, g_ref, gw1_ref, gw2_ref, gb1_ref, gx_ref, y_ref, vec_ref,
                  gq, gk, gv, go, bq, bv, w1_out, b1_out, w2_out, x_out, y_out, *vec_outs):
    hw = heads * hd
    for i, out in enumerate((gq, gk, gv, go)):
        out[...] = g_ref[i * hw:(i + 1) * hw]
    sums = g_ref[4 * hw:].astype(F32)[:1]
    for i, out in ((0, bq), (2, bv)):
        for h in range(heads):
            at = i * hw + h * hd
            out[h:h + 1] = sums[:, at:at + hd].astype(BF16)
    w1_out[...] = gw1_ref[...].T
    b1_out[...] = gb1_ref[0].astype(BF16)
    w2_out[...] = gw2_ref[...]
    x_out[...] = gx_ref[...]
    y_out[...] = y_ref[...]
    for i, out in enumerate(vec_outs):
        out[...] = vec_ref[i].astype(out.dtype)


def finish(g, gw1, gw2, gb1, gx, y, vec, heads, hd):
    width = g.shape[1]
    mlp = gw2.shape[0]
    hw = heads * hd
    bf = lambda *shape: jax.ShapeDtypeStruct(shape, BF16)
    f32_row = jax.ShapeDtypeStruct((width,), F32)
    vm = pl.BlockSpec(memory_space=pltpu.VMEM)
    outs = [bf(hw, width)] * 4 + [bf(heads, hd)] * 2 + [bf(width, mlp), bf(mlp), bf(mlp, width), bf(*gx.shape), bf(*y.shape)]
    outs += [f32_row] * 4 + [bf(width)] * 2
    return pl.pallas_call(
        functools.partial(finish_kernel, heads, hd),
        in_specs=[vm] * 7,
        out_specs=[vm] * len(outs),
        out_shape=outs,
        compiler_params=pltpu.CompilerParams(vmem_limit_bytes=67_043_328),
        name="finish",
    )(g, gw1, gw2, gb1, gx, y, vec)


def solution(mesh):
    act_spec = P('dp', 'tp', None)
    replicated = P()
    head_w = P(None, 'tp', None)
    head_b = P('tp', None)
    grad_head_w = P('dp', 'tp', None)
    grad_head_b = P(('dp', 'tp'), None)
    grad_vec = P('dp')
    in_specs = (act_spec, act_spec, replicated, replicated, head_w, head_b, head_w, head_w, head_b,
                P('tp', None, None), replicated, replicated, replicated, P(None, 'tp'), P('tp'), P('tp', None), replicated)
    out_specs = (act_spec, act_spec, grad_vec, grad_vec, grad_head_w, grad_head_b, grad_head_w, grad_head_w, grad_head_b,
                 P(('dp', 'tp'), None, None), grad_vec, grad_vec, grad_vec, P('dp', 'tp'), P(('dp', 'tp')),
                 P(('dp', 'tp'), None), grad_vec)

    def layer_step(x, d_out, ln1_gain, ln1_bias, w_q, b_q, w_k, w_v, b_v, w_o, b_o, ln2_gain, ln2_bias, w_1, b_1, w_2, b_2):
        width = x.shape[-1]
        heads_loc, hd = w_q.shape[1:]
        hw = heads_loc * hd
        flat = lambda w: w.transpose(1, 2, 0).reshape(hw, width)
        qkv, mixed, stats, h_one, y_img, d_mid, sums, w1t, x_img, wcat, d_out_all, h2_all = front(
            x, (flat(w_q), flat(w_k), flat(w_v), w_o.reshape(hw, width)), (b_q, b_v, b_1),
            (ln1_gain[None], ln1_bias[None], ln2_gain[None], ln2_bias[None]), (b_o, b_2), w_1, w_2, d_out, heads_loc, hd)
        g_all, gw1, gw2, gb1, gx, vec, y_tok = back(
            h_one, d_mid, wcat, qkv, mixed, stats, h2_all, d_out_all, w1t, w_2, x_img, y_img, ln1_gain[None], sums, heads_loc, hd)
        (gq, gk, gv, go, grad_b_q, grad_b_v, grad_w_1, grad_b_1, grad_w_2, grad_x, y_out, g_ln1_gain, g_ln1_bias, g_ln2_gain, g_ln2_bias,
         grad_b_o, grad_b_2) = finish(g_all, gw1, gw2, gb1, gx, y_tok, vec, heads_loc, hd)
        gq, gk, gv = (z.reshape(heads_loc, hd, width).transpose(2, 0, 1) for z in (gq, gk, gv))
        grad_w_o = go.reshape(w_o.shape)
        return (y_out, grad_x, g_ln1_gain, g_ln1_bias, gq, grad_b_q, gk, gv, grad_b_v, grad_w_o,
                grad_b_o, g_ln2_gain, g_ln2_bias, grad_w_1, grad_b_1, grad_w_2, grad_b_2)

    return jax.shard_map(layer_step, mesh=mesh, in_specs=in_specs, out_specs=out_specs, check_vma=False)
```

time: 349 us -> 321 us (0.920)
  local copies, waits for them, and re-layouts: 21.8 us -> 0 us
    unnamed x27 -> x0, local copies, waits for them, and re-layouts: 10.9 us -> none
    slice x4 -> x0, local copies, waits for them, and re-layouts: 4.18 us -> none  [the longest x1 2.26 us: layer_step(): grad_w_o = g_all[3 * hw:4 * hw].reshape(w_o.shape)]
    pallas_call x2 -> x3, Pallas kernels: 323 us -> 320 us  [the longest x1 206 us: front(): pl.pallas_call(functools.partial(front_kernel, heads, hd, size), grid=(2...]
where the time goes in v3:
time: 321 us
  Pallas kernels  320 us (100%)
    pallas_call x1, Pallas kernels, front(): pl.pallas_call(functools.partial(front_kernel, heads, hd, size), grid=(2...  206 us
    pallas_call x1, Pallas kernels, back(): pl.pallas_call(functools.partial(back_kernel, heads, hd, size), grid=(2 *...  109 us

profile of v3, /device:TPU:81, one launch (start us, length us, event | category | flops | bytes accessed | tf_op | source)
XLA Modules:
  0.0 320.9 jit_solution(17388457572453969670)
XLA Ops:
  0.7 205.5 %front.1 = (bf16[8,384,576]{2,1,0:T(8,128)(2,1)}, bf16[8,128,576]{2,1,0:T(8,128)(2,1)}, f32[8,4,576]{2,1,0:T(4,128)}, bf16[576,1024]{1,0:T(8,128)(2,1)}, bf16[57...) custom-call(bf16[8,72,1024]{2,1,0:T(8,128)(2,1)} %x_ref.1, ...), custom_call_target="tpu_custom_call" | custom-call | tf_op jit(solution)/shard_map/front/pallas_call | solution.py:382
  206.2 109.2 %back.1 = (bf16[528,1024]{1,0:T(8,128)(2,1)}, bf16[512,1024]{1,0:T(8,128)(2,1)}, bf16[512,1024]{1,0:T(8,128)(2,1)}, f32[8,512]{1,0:T(8,128)}, bf16[8,72,1024]{2,...) custom-call(bf16[576,1024]{1,0:T(8,128)(2,1)} %get-tuple-element.53.h_ref, ...), custom_call_target="tpu_custom_call" | custom-call | tf_op jit(solution)/shard_map/back/pallas_call | solution.py:625
  315.4 5.4 %finish.1 = (bf16[128,1024]{1,0:T(8,128)(2,1)}, bf16[128,1024]{1,0:T(8,128)(2,1)}, bf16[128,1024]{1,0:T(8,128)(2,1)}, bf16[128,1024]{1,0:T(8,128)(2,1)}, bf16[2,...) custom-call(bf16[528,1024]{1,0:T(8,128)(2,1)} %get-tuple-element.65., ...), custom_call_target="tpu_custom_call" | custom-call | tf_op jit(solution)/shard_map/finish/pallas_call | solution.py:673

commit v4 on v3

--- a/solution.py
+++ b/solution.py
@@ -176,8 +176,8 @@
 
 def front_kernel(heads, hd, size, x_ref, wq_ref, wk_ref, wv_ref, wo_ref, bq_ref, bv_ref, b1_ref,
                  g1_ref, c1_ref, g2_ref, c2_ref, bo_ref, b2_ref, w1_ref, w2_ref, do_ref,
-                 qkv_ref, mix_ref, st_ref, h1_ref, y_ref, dm_ref, sums_ref, w1t_ref, xi_ref, wa_ref, doa_ref, h2a_ref,
-                 wl_ref, w_all, w1_all, w2_all, x_all, via, acc_ref, dacc, own_do, d_img, xm_ref, h2_ref, loc_sem, out_sem, send_sem, recv_sem):
+                 qkv_ref, mix_ref, st_ref, h1_out, y_out, dm_out, sums_ref, w1t_out, xi_ref, wa_ref, doa_ref, h2a_ref,
+                 h1_ref, y_ref, dm_ref, w1t_ref, wl_ref, w_all, w1_all, w2_all, x_all, via, acc_ref, dacc, own_do, d_img, xm_ref, h2_ref, loc_sem, out_sem, send_sem, recv_sem):
     hw = heads * hd
     scale = 1.0 / math.sqrt(hd)
     step = pl.program_id(0)
@@ -202,6 +202,7 @@
     in_x, in_do = local(x_ref.at[me], x_all.at[me], 0), local(do_ref, own_do, 1)
     out_w, out_h2 = local(wl_ref, wa_ref.at[me], 2), local(h2_ref, h2a_ref.at[me], 3)
     in_img = local(doa_ref.at[me], d_img, 6)
+    out_h1, out_w1t, out_y, out_dm = local(h1_ref, h1_out, 7), local(w1t_ref, w1t_out, 8), local(y_ref, y_out, 9), local(dm_ref, dm_out, 10)
     out_x, out_do = local(x_all, xi_ref, 4), local(own_do, doa_ref.at[:, mine(me)], 5)
 
     def out_block(i):
@@ -296,7 +297,7 @@
         in_img.start()
         in_img.wait()
 
-    gw1.follow(k)
+    gw1.follow(k, out_h1.start, out_w1t.start)
     gw2.follow(k, gw2.forward, gh2.start)
 
     @pl.when(k >= 0)
@@ -335,14 +336,16 @@
             for i, v in enumerate((dh * xhat, dh, dm.astype(F32), do)):
                 sums_ref[2 + i:3 + i] += jnp.sum(v, axis=0, keepdims=True)
 
+        gh2.forward()
         pair_chunks(size, tok, body)
-        gh2.forward()
         gh2.near()
+        out_y.start()
+        out_dm.start()
         gh2.far()
         gh2.received(*range(6, Gather.COPIES))
         for g in (gw, gw1, gdo, gw2, gh2):
             g.sent()
-        for c in (out_x, out_w, out_h2):
+        for c in (out_x, out_w, out_h2, out_h1, out_w1t, out_y, out_dm):
             c.wait()
         for i in range(1, size):
             out_block(i).wait()
@@ -383,14 +386,14 @@
         functools.partial(front_kernel, heads, hd, size),
         grid=(2 * size,),
         in_specs=[ANY] + [whole(*z.shape) for z in weights + biases + gains + sums_bias] + [ whole(width, mlp), whole(mlp, width), ANY],
-        out_specs=[block(order, 3 * hw, n), block(order, hw, n), block(order, 2 * heads, n), whole(n, width), whole(n, width),
-                   whole(n, width), whole(8, width), whole(mlp, width), ANY, ANY, ANY, ANY],
+        out_specs=[block(order, 3 * hw, n), block(order, hw, n), block(order, 2 * heads, n), ANY, ANY, ANY, whole(8, width)]
+                  + [ANY] * 5,
         out_shape=[bf(size, 3 * hw, n), bf(size, hw, n), jax.ShapeDtypeStruct((size, 2 * heads, n), F32), bf(n, width), bf(n, width),
                    bf(n, width), jax.ShapeDtypeStruct((8, width), F32), bf(mlp, width),
                    bf(size, tok, width), bf(size, rows, width), bf(imgs, n, width), bf(size, n, width)],
-        scratch_shapes=[buf(rows, width), buf(size, rows, width), buf(size, width, mlp), buf(size, mlp, width), buf(size, tok, width), buf(2, tok, width),
+        scratch_shapes=[buf(n, width), buf(n, width), buf(n, width), buf(mlp, width), buf(rows, width), buf(size, rows, width), buf(size, width, mlp), buf(size, mlp, width), buf(size, tok, width), buf(2, tok, width),
                         pltpu.VMEM((n, width), F32), pltpu.VMEM((n, width), F32), buf(*d_out.shape), buf(n, width), buf(n, width),
-                        buf(n, width), dma(7), dma(size), dma(copies), dma(copies)],
+                        buf(n, width), dma(11), dma(size), dma(copies), dma(copies)],
         compiler_params=kernel_params(1),
         name="front",
     )(x, *weights, *biases, *gains, *sums_bias, w_1, w_2, d_out)
@@ -406,9 +409,10 @@
     return 2 * chip + side
 
 
-def back_kernel(heads, hd, size, h_ref, dm_ref, w_ref, qkv_ref, mix_ref, st_ref, h2_ref, do_ref, w1_ref, w2_ref, b_ref,
-                x3_ref, dm3_ref, y3_ref, gain_ref, vin_ref,
-                g_ref, gw1_ref, gw2_ref, gb1_ref, gx_ref, vec_ref, yo_ref,
+def back_kernel(heads, hd, size, h_ref, dm_ref, w_ref, qkv_ref, mix_ref, st_ref, h2_ref, do_ref, w1_in, w2_in, b_ref,
+                x3_in, dm3_in, y3_ref, gain_ref, vin_ref,
+                g_out, gw1_out, gw2_out, gb1_ref, gx_ref, vec_ref, yo_ref,
+                w1_ref, w2_ref, x3_ref, dm3_ref, g_ref, gw1_ref, gw2_ref,
                 dqkv_ref, dh_ref, gx_own, v_own, v_all, via_y, via_g,
                 outs, pair_in, opp_l, opp_r, near_l, near_r, acc, loc_sem, send_sem, recv_sem):
     hw = heads * hd
@@ -431,6 +435,8 @@
     base += Exchange.COPIES
     local = lambda src, dst, i: pltpu.make_async_copy(src, dst, loc_sem.at[i])
     y_local, gx_local = local(y3_ref.at[me], yo_ref.at[me], 1), local(gx_own.at[me], gx_ref.at[me], 2)
+    late = [local(src, dst, 3 + i) for i, (src, dst) in enumerate(((x3_in, x3_ref), (dm3_in, dm3_ref), (w1_in, w1_ref), (w2_in, w2_ref)))]
+    outward = [local(src, dst, 7 + i) for i, (src, dst) in enumerate(((gw1_ref, gw1_out), (gw2_ref, gw2_out), (g_ref, g_out)))]
 
     def numbered(src, dst, i, dev):
         return push(src, dst, send_sem.at[base + i], recv_sem.at[base + i], dev)
@@ -456,6 +462,8 @@
         greet_all(size)
         ex_y.start()
         y_local.start()
+        for c in late:
+            c.start()
 
     @pl.when(j == 1)
     def _():
@@ -540,6 +548,8 @@
     @pl.when(m == 0)
     def _():
         v_own[...] = vin_ref[...]
+        for c in late:
+            c.wait()
 
         @pl.loop(0, size)
         def _(dev):
@@ -592,6 +602,8 @@
         ring_copies = (right_hi(), right_lo(), left_lo(), left_hi())
         for c in ring_copies:
             c.wait_recv()
+        outward[0].start()
+        outward[1].start()
         g_ref[...] = (outs[own] + near_l[...] + near_r[...]).astype(BF16)
         for c in ring_copies + (pair_copy(pairs - 2), pair_copy(pairs - 1)):
             c.wait_send()
@@ -602,10 +614,13 @@
         for i in range(1, size):
             total += v_all[i]
         vec_ref[...] = total
+        outward[2].start()
         ex_y.close()
         ex_g.close()
         gx_local.wait()
         y_local.wait()
+        for c in outward:
+            c.wait()
 
 
 def back(h_one, d_mid, wcat, qkv, mix, stats, h2_all, d_out_all, w1t, w_2, x3, y_img, gain, sums, heads, hd):
@@ -626,16 +641,17 @@
         functools.partial(back_kernel, heads, hd, size),
         grid=(2 * size,),
         in_specs=[whole(n, width), whole(n, width), block(first, rows, width), block(first, 3 * hw, n), block(first, hw, n),
-                  block(first, 2 * heads, n), block(second, n, width), block(second, n, width), whole(mlp, width), whole(mlp, width),
+                  block(first, 2 * heads, n), block(second, n, width), block(second, n, width), ANY, ANY,
                   pl.BlockSpec((1, BIAS_ROWS, width), lambda i: (lax.axis_index('tp'), rows // BIAS_ROWS - 1, 0)),
-                  act3, act3, act3, whole(1, width), whole(*sums.shape)],
-        out_specs=[whole(rows, width), whole(mlp, width), whole(mlp, width), whole(8, mlp), ANY, whole(*sums.shape), ANY],
+                  ANY, ANY, act3, whole(1, width), whole(*sums.shape)],
+        out_specs=[ANY, ANY, ANY, whole(8, mlp), ANY, whole(*sums.shape), ANY],
         out_shape=[bf(rows, width), bf(mlp, width), bf(mlp, width), jax.ShapeDtypeStruct((8, mlp), F32), bf(*x3.shape),
                    jax.ShapeDtypeStruct(sums.shape, F32), bf(*x3.shape)],
-        scratch_shapes=[half_buf(3 * hw, n), buf(n, width), half_buf(*x3.shape), buf(*sums.shape), buf(size, *sums.shape),
+        scratch_shapes=[half_buf(mlp, width), half_buf(mlp, width), half_buf(*x3.shape), half_buf(*x3.shape), half_buf(rows, width),
+                        half_buf(mlp, width), half_buf(mlp, width), half_buf(3 * hw, n), buf(n, width), half_buf(*x3.shape), buf(*sums.shape), buf(size, *sums.shape),
                         half_buf(2, *tokens), half_buf(2, *tokens), buf(size // 2 + 1, rows, width), buf(2, rows, width),
                         buf(half, width), buf(rows - half, width), buf(rows, width), buf(rows, width), buf(2 * mlp, width),
-                        dma(3), dma(copies), dma(copies)],
+                        dma(10), dma(copies), dma(copies)],
         compiler_params=kernel_params(2),
         name="back",
     )(h_one, d_mid, wcat, qkv, mix, stats, h2_all, d_out_all, w1t, w_2, wcat, x3, d_mid.reshape(x3.shape), y_img.reshape(x3.shape),

time: 321 us -> 317 us (0.988)
  Pallas kernels: 320 us -> 316 us
where the time goes in v4:
time: 317 us
  Pallas kernels  316 us (100%)
    pallas_call x1, Pallas kernels, front(): pl.pallas_call(functools.partial(front_kernel, heads, hd, size), grid=(2...  204 us
    pallas_call x1, Pallas kernels, back(): pl.pallas_call(functools.partial(back_kernel, heads, hd, size), grid=(2 *...  107 us

profile of v4, /device:TPU:81, one launch (start us, length us, event | category | flops | bytes accessed | tf_op | source)
XLA Modules:
  0.0 316.9 jit_solution(15983838299484382641)
XLA Ops:
  0.7 204.1 %front.1 = (bf16[8,384,576]{2,1,0:T(8,128)(2,1)}, bf16[8,128,576]{2,1,0:T(8,128)(2,1)}, f32[8,4,576]{2,1,0:T(4,128)}, bf16[576,1024]{1,0:T(8,128)(2,1)}, bf16[57...) custom-call(bf16[8,72,1024]{2,1,0:T(8,128)(2,1)} %x_ref.1, ...), custom_call_target="tpu_custom_call" | custom-call | tf_op jit(solution)/shard_map/front/pallas_call | solution.py:385
  204.8 106.6 %back.1 = (bf16[528,1024]{1,0:T(8,128)(2,1)}, bf16[512,1024]{1,0:T(8,128)(2,1)}, bf16[512,1024]{1,0:T(8,128)(2,1)}, f32[8,512]{1,0:T(8,128)}, bf16[8,72,1024]{2,...) custom-call(bf16[576,1024]{1,0:T(8,128)(2,1)} %get-tuple-element.53.h_ref, ...), custom_call_target="tpu_custom_call" | custom-call | tf_op jit(solution)/shard_map/back/pallas_call | solution.py:640
  311.4 5.4 %finish.1 = (bf16[128,1024]{1,0:T(8,128)(2,1)}, bf16[128,1024]{1,0:T(8,128)(2,1)}, bf16[128,1024]{1,0:T(8,128)(2,1)}, bf16[128,1024]{1,0:T(8,128)(2,1)}, bf16[2,...) custom-call(bf16[528,1024]{1,0:T(8,128)(2,1)} %get-tuple-element.65., ...), custom_call_target="tpu_custom_call" | custom-call | tf_op jit(solution)/shard_map/finish/pallas_call | solution.py:689

commit v5 on v4

--- a/solution.py
+++ b/solution.py
@@ -559,9 +559,9 @@
             v_own[0:1] += jnp.sum(dh * xhat, axis=0, keepdims=True)
             v_own[1:2] += jnp.sum(dh, axis=0, keepdims=True)
 
+        ex_g.start()
         for r in range(1, size):
             v_copy(lax.rem(me + r, size), me).start()
-        ex_g.start()
         gx_local.start()
         v_all[me] = v_own[...]
 

time: 317 us -> 317 us (level)
  no operation moved by 1% of the time
where the time goes in v5:
time: 317 us
  Pallas kernels  316 us (100%)
    pallas_call x1, Pallas kernels, front(): pl.pallas_call(functools.partial(front_kernel, heads, hd, size), grid=(2...  204 us
    pallas_call x1, Pallas kernels, back(): pl.pallas_call(functools.partial(back_kernel, heads, hd, size), grid=(2 *...  107 us

profile of v5, /device:TPU:81, one launch (start us, length us, event | category | flops | bytes accessed | tf_op | source)
XLA Modules:
  0.0 316.9 jit_solution(3986899870689921094)
XLA Ops:
  0.7 204.1 %front.1 = (bf16[8,384,576]{2,1,0:T(8,128)(2,1)}, bf16[8,128,576]{2,1,0:T(8,128)(2,1)}, f32[8,4,576]{2,1,0:T(4,128)}, bf16[576,1024]{1,0:T(8,128)(2,1)}, bf16[57...) custom-call(bf16[8,72,1024]{2,1,0:T(8,128)(2,1)} %x_ref.1, ...), custom_call_target="tpu_custom_call" | custom-call | tf_op jit(solution)/shard_map/front/pallas_call | solution.py:385
  204.8 106.6 %back.1 = (bf16[528,1024]{1,0:T(8,128)(2,1)}, bf16[512,1024]{1,0:T(8,128)(2,1)}, bf16[512,1024]{1,0:T(8,128)(2,1)}, f32[8,512]{1,0:T(8,128)}, bf16[8,72,1024]{2,...) custom-call(bf16[576,1024]{1,0:T(8,128)(2,1)} %get-tuple-element.53.h_ref, ...), custom_call_target="tpu_custom_call" | custom-call | tf_op jit(solution)/shard_map/back/pallas_call | solution.py:640
  311.4 5.4 %finish.1 = (bf16[128,1024]{1,0:T(8,128)(2,1)}, bf16[128,1024]{1,0:T(8,128)(2,1)}, bf16[128,1024]{1,0:T(8,128)(2,1)}, bf16[128,1024]{1,0:T(8,128)(2,1)}, bf16[2,...) custom-call(bf16[528,1024]{1,0:T(8,128)(2,1)} %get-tuple-element.65., ...), custom_call_target="tpu_custom_call" | custom-call | tf_op jit(solution)/shard_map/finish/pallas_call | solution.py:689
